TPU v7x, 32 devices: a 4x2x2 block of a 4x4x8 slice. The times are simulated.
32 devices in a mesh: dp: 4 (over y, z), sp: 8 (over x, core).
Axes of the slice: x: 4, y: 2, z: 2, core: 2. Of those that a mesh axis runs over, the one named last changes fastest.
The devices are a block of a 4x4x8 slice.
Arguments:
- prompt: bfloat16 [32, 2048, 2048], P('dp', 'sp'), parts along dimension 0
- w_q: bfloat16 [2048, 2048], replicated
- w_k: bfloat16 [2048, 2048], replicated
- w_v: bfloat16 [2048, 2048], replicated
- w_o: bfloat16 [2048, 2048], replicated
- q_norm_w: float32 [2048], replicated
- k_norm_w: float32 [2048], replicated
- post_norm_w: float32 [2048], replicated
- new_token: bfloat16 [32, 2048], P('dp'), parts along dimension 0
Outputs:
- output 1: bfloat16 [32, 2048, 2048], P('dp', 'sp'), parts along dimension 0
- output 2: bfloat16 [32, 2049, 16, 128], P('dp', None, 'sp'), parts along dimension 0
- output 3: bfloat16 [32, 2049, 16, 128], P('dp', None, 'sp'), parts along dimension 0
- output 4: bfloat16 [32, 2048], P('dp'), parts along dimension 0
There are 4 independent parts. A program takes and returns all parts, laid end to end along the dimension named above; an argument that names none is the same for every part.
All inputs are finite; a program needn't handle non-finite values.
Results may differ from a plain program's by a relative error of at most 0.00731166.
Values are sent between devices in bfloat16 or wider.
A program may use at most 768 MiB of HBM per device.

v0:
```python
import jax
import jax.numpy as jnp
from jax import lax
from jax.sharding import PartitionSpec as P

HEAD_DIM = 128
ROPE_THETA = 500000.0
NORM_EPS = 1e-6


def rms_norm(values, weight):
    return values * lax.rsqrt(jnp.mean(values * values, axis=-1, keepdims=True) + NORM_EPS) * weight


def rope_tables(positions):
    inv_freq = ROPE_THETA ** (-jnp.arange(0, HEAD_DIM, 2).astype(jnp.float32) / HEAD_DIM)
    angles = positions.astype(jnp.float32)[:, None] * inv_freq[None, :]
    angles = jnp.concatenate([angles, angles], axis=-1)
    return jnp.cos(angles), jnp.sin(angles)


def apply_rope(values, cos_t, sin_t):
    half_dim = HEAD_DIM // 2
    rotated = jnp.concatenate([-values[..., half_dim:], values[..., :half_dim]], axis=-1)
    return values * cos_t[:, None, :] + rotated * sin_t[:, None, :]


def project_heads(x_rows, w_mat, norm_w, cos_t, sin_t):
    normed = rms_norm(jnp.dot(x_rows, w_mat, preferred_element_type=jnp.float32), norm_w)
    return apply_rope(normed.reshape(x_rows.shape[:-1] + (-1, HEAD_DIM)), cos_t, sin_t).astype(jnp.bfloat16)


def causal_attention(q_loc, k_all, v_all, q_start):
    n_batch, tok_len, n_heads, head_dim = q_loc.shape
    block_rows = min(tok_len, 128)
    key_pos = jnp.arange(k_all.shape[1])
    score_scale = head_dim ** -0.5

    def one_block(block_idx):
        q_blk = lax.dynamic_slice_in_dim(q_loc, block_idx * block_rows, block_rows, axis=1)
        q_pos = q_start + block_idx * block_rows + jnp.arange(block_rows)
        scores = jnp.einsum("bqhd,bkhd->bhqk", q_blk, k_all, preferred_element_type=jnp.float32) * score_scale
        scores = jnp.where((q_pos[:, None] >= key_pos[None, :])[None, None], scores, -1e30)
        attn_p = jax.nn.softmax(scores, axis=-1).astype(jnp.bfloat16)
        return jnp.einsum("bhqk,bkhd->bqhd", attn_p, v_all, preferred_element_type=jnp.float32).astype(jnp.bfloat16)

    blocks = lax.map(one_block, jnp.arange(tok_len // block_rows))
    return jnp.moveaxis(blocks, 0, 1).reshape(n_batch, tok_len, n_heads * head_dim)


def solution(mesh):
    group_n = mesh.shape["sp"]

    def device_step(prompt_blk, w_q, w_k, w_v, w_o, q_norm_w, k_norm_w, post_norm_w, new_rows):
        n_batch, tok_len, full_width = prompt_blk.shape
        n_heads = full_width // HEAD_DIM
        heads_loc = n_heads // group_n
        cols_loc = heads_loc * HEAD_DIM
        my_index = lax.axis_index("sp")
        q_start = my_index * tok_len
        cos_p, sin_p = rope_tables(q_start + jnp.arange(tok_len))
        q_loc = project_heads(prompt_blk, w_q, q_norm_w, cos_p, sin_p)
        k_loc = project_heads(prompt_blk, w_k, k_norm_w, cos_p, sin_p)
        v_loc = jnp.dot(prompt_blk, w_v, preferred_element_type=jnp.float32).astype(jnp.bfloat16).reshape(n_batch, tok_len, n_heads, HEAD_DIM)
        k_all = lax.all_gather(k_loc, "sp", axis=1, tiled=True)
        v_all = lax.all_gather(v_loc, "sp", axis=1, tiled=True)
        attn_out = causal_attention(q_loc, k_all, v_all, q_start)
        proj_pre = jnp.dot(attn_out, w_o, preferred_element_type=jnp.float32)
        out_p = (prompt_blk.astype(jnp.float32) + rms_norm(proj_pre, post_norm_w)).astype(jnp.bfloat16)
        k_mine = lax.dynamic_slice_in_dim(k_all, my_index * heads_loc, heads_loc, axis=2)
        v_mine = lax.dynamic_slice_in_dim(v_all, my_index * heads_loc, heads_loc, axis=2)
        col_start = my_index * cols_loc
        q_raw = jnp.dot(new_rows, lax.dynamic_slice_in_dim(w_q, col_start, cols_loc, axis=1), preferred_element_type=jnp.float32)
        k_raw = jnp.dot(new_rows, lax.dynamic_slice_in_dim(w_k, col_start, cols_loc, axis=1), preferred_element_type=jnp.float32)
        v_new = jnp.dot(new_rows, lax.dynamic_slice_in_dim(w_v, col_start, cols_loc, axis=1), preferred_element_type=jnp.float32).astype(jnp.bfloat16).reshape(n_batch, heads_loc, HEAD_DIM)
        sq_sums = jnp.stack([jnp.sum(q_raw * q_raw, axis=-1), jnp.sum(k_raw * k_raw, axis=-1)], axis=-1)
        sq_total = lax.psum(sq_sums, "sp")
        cos_d, sin_d = rope_tables(jnp.full((1,), tok_len * group_n))
        q_scaled = q_raw * lax.rsqrt(sq_total[:, 0:1] / full_width + NORM_EPS) * lax.dynamic_slice_in_dim(q_norm_w, col_start, cols_loc)
        k_scaled = k_raw * lax.rsqrt(sq_total[:, 1:2] / full_width + NORM_EPS) * lax.dynamic_slice_in_dim(k_norm_w, col_start, cols_loc)
        q_new = apply_rope(q_scaled.reshape(n_batch, heads_loc, HEAD_DIM), cos_d, sin_d).astype(jnp.bfloat16)
        k_new = apply_rope(k_scaled.reshape(n_batch, heads_loc, HEAD_DIM), cos_d, sin_d).astype(jnp.bfloat16)
        k_cache = jnp.concatenate([k_mine, k_new[:, None]], axis=1)
        v_cache = jnp.concatenate([v_mine, v_new[:, None]], axis=1)
        scores = jnp.einsum("bhd,bkhd->bhk", q_new, k_cache, preferred_element_type=jnp.float32) * HEAD_DIM ** -0.5
        attn_d = jax.nn.softmax(scores, axis=-1).astype(jnp.bfloat16)
        o_new = jnp.einsum("bhk,bkhd->bhd", attn_d, v_cache, preferred_element_type=jnp.float32).astype(jnp.bfloat16).reshape(n_batch, cols_loc)
        part_proj = jnp.dot(o_new, lax.dynamic_slice_in_dim(w_o, col_start, cols_loc, axis=0), preferred_element_type=jnp.float32).astype(jnp.bfloat16)
        all_parts = lax.all_gather(part_proj, "sp")
        proj_new = jnp.sum(all_parts.astype(jnp.float32), axis=0)
        out_d = (new_rows.astype(jnp.float32) + rms_norm(proj_new, post_norm_w)).astype(jnp.bfloat16)
        return out_p, k_cache, v_cache, out_d

    replicated = P()
    return jax.shard_map(
        device_step, mesh=mesh,
        in_specs=(P("dp", "sp", None), replicated, replicated, replicated, replicated, replicated, replicated, replicated, P("dp", None)),
        out_specs=(P("dp", "sp", None), P("dp", None, "sp", None), P("dp", None, "sp", None), P("dp", None)),
        check_vma=False)
```

profile of v0, /device:TPU:81, one launch (start us, length us, event | category | flops | bytes accessed | tf_op | source)
XLA Modules:
  0.0 1121.6 jit_solution(3501534942379759904)
XLA Ops:
  7.2 0.1 all-gather.6.cloned.1.call-start
  7.2 23.5 %fusion.37 = bf16[8,256,2048]{2,1,0:T(8,128)(2,1)} fusion(bf16[8,256,2048]{2,1,0:T(8,128)(2,1)} %param.11, bf16[2048,2048]{1,0:T(8,128)(2,1)} %param.14), kind=kOutput, calls=%fused_computation.50 | convolution fusion | flops 17184063488 | bytes 25165824 | tf_op jit(solution)/shard_map/dot_general | solution.py:64
  30.8 9.8 copy.47
  40.6 0.1 all-gather.6.cloned.1.call-update
  40.7 0.5 all-gather.4.cloned.1.call-start
  41.2 0.0 copy-start.8
  41.2 21.8 %multiply_reduce_fusion.2 = (f32[8,256]{1,0:T(8,128)S(1)}, f32[8,256,2048]{2,1,0:T(8,128)S(1)}) fusion(bf16[8,256,2048]{2,1,0:T(8,128)(2,1)} %param.11, bf16[2048,2048]{1,0:T(8,128)(2,1)} %param.12), kind=kOutput, calls=%fused_computation.35 | convolution fusion | flops 17188255744 | bytes 33562624 | tf_op jit(solution)/shard_map/dot_general | solution.py:29
  63.1 1.6 multiply_multiply_fusion.1
  64.7 7.3 copy.45
  72.1 21.8 %multiply_reduce_fusion.1 = (f32[8,256]{1,0:T(8,128)S(1)}, f32[8,256,2048]{2,1,0:T(8,128)S(1)}) fusion(bf16[8,256,2048]{2,1,0:T(8,128)(2,1)} %param.11, bf16[2048,2048]{1,0:T(8,128)(2,1)} %param.13), kind=kOutput, calls=%fused_computation.33 | convolution fusion | flops 17188255744 | bytes 33562624 | tf_op jit(solution)/shard_map/dot_general | solution.py:29
  93.9 1.7 multiply_multiply_fusion
  95.6 7.4 copy.46
  103.0 0.1 broadcast_multiply_fusion
  103.1 0.5 fusion.55
  103.7 45.7 %slice_negate_fusion = (f32[8,256,16,64]{3,2,1,0:T(8,128)}, f32[8,256,16,64]{3,2,1,0:T(8,128)}, f32[8,256,16,64]{3,2,1,0:T(8,128)}, f32[8,256,16,64]{3,2,1,0:T(8,128)}) fusion(f32[8,256,16,128]{3,2,1,0:T(8,128)} %bitcast.113, f32[8,256,16,128]{3,2,1,0:T(8,128)} %bitcast.111), kind=kLoop, calls=%fused_computation.22 | loop fusion | flops 4194304 | bytes 67108864 | tf_op jit(solution)/shard_map/neg | solution.py:24
  149.3 39.3 %fusion.24 = (bf16[8,256,16,128]{3,2,1,0:T(8,128)(2,1)}, bf16[8,256,16,128]{3,2,1,0:T(8,128)(2,1)}) fusion(f32[8,256,16,64]{3,2,1,0:T(8,128)} %get-tuple-element.101, f32[8,256,16,64]{3,2,1,0:T(8,128)} %get-tuple-element.100, f32[256,128]{1,0:T(8,128)S(1)} %get-tuple-element.107, f32[256,128]{1,0:T(8,128)S(1)} %get-tuple-element.106, ...), kind=kLoop, calls=%fused_computation.29 | loop fusion | flops 41943040 | bytes 84148224 | tf_op jit(solution)/shard_map/convert_element_type | solution.py:30
  188.6 0.1 all-gather.4.cloned.1.call-update
  188.7 0.1 dynamic_slice.37
  188.8 0.1 dynamic_slice.34
  188.8 1.5 fusion.45
  190.3 0.6 copy.35
  190.9 1.6 multiply_reduce_fusion.5
  192.5 1.6 multiply_reduce_fusion.4
  194.1 14.5 %psum.7 = f32[8,2]{0,1:T(2,128)S(1)} all-reduce(f32[8,2]{0,1:T(2,128)S(1)} %pad_maximum_fusion.3), channel_id=1, replica_groups=mesh['dp'=4,'sp'=8] {'sp'}, use_global_device_ids=true, to_apply=%region_9.10 | all-reduce | flops 16 | bytes 128 | tf_op jit(solution)/shard_map/psum | solution.py:77
  208.6 0.1 fusion.73
  208.8 0.1 fusion.63
  208.8 0.1 slice_negate_fusion.3
  208.9 0.7 fusion.58
  209.6 0.1 multiply_bitcast_fusion
  209.7 0.1 slice_negate_fusion.2
  209.8 0.7 fusion.64
  210.4 129.3 %all-gather.6.cloned.1.call-done = bf16[8,2048,16,128]{3,2,1,0:T(8,128)(2,1)} async-done(((bf16[8,256,16,128]{3,2,1,0:T(8,128)(2,1)}), bf16[8,2048,16,128]{3,2,1,0:T(8,128)(2,1)}) %all-gather.6.cloned.1.call-update) | async-done | bytes 67108880 | tf_op jit(solution)/shard_map/all_gather | solution.py:66
  339.8 44.6 %copy.30 = bf16[8,2048,16,128]{3,1,2,0:T(8,128)(2,1)} copy(bf16[8,2048,16,128]{3,2,1,0:T(8,128)(2,1)} %all-gather.6.cloned.1.call-done) | data formatting | bytes 134217728
  384.4 252.2 %all-gather.4.cloned.1.call-done = bf16[8,2048,16,128]{3,2,1,0:T(8,128)(2,1)} async-done(((bf16[8,256,16,128]{3,2,1,0:T(8,128)(2,1)}), bf16[8,2048,16,128]{3,2,1,0:T(8,128)(2,1)}) %all-gather.4.cloned.1.call-update) | async-done | bytes 67108880 | tf_op jit(solution)/shard_map/all_gather | solution.py:65
  636.6 44.7 %copy.29 = bf16[8,2048,16,128]{3,1,2,0:T(8,128)(2,1)} copy(bf16[8,2048,16,128]{3,2,1,0:T(8,128)(2,1)} %all-gather.4.cloned.1.call-done) | data formatting | bytes 134217728
  681.3 287.3 %while.11 = (s32[]{:T(128)}, bf16[2,8,128,16,128]{4,2,3,1,0:T(8,128)(2,1)}, s32[2]{0:T(128)S(1)}, s32[]{:T(128)}, bf16[8,256,16,128]{3,2,1,0:T(8,128)(2,1)}, /*i...) while((s32[]{:T(128)}, ...), condition=%wide.region_5.6_spmd.clone, body=%wide.region_2.5_spmd.clone.sunk | while | flops 17383557120 | bytes 420087104 | solution.py:47
  681.3 0.6 dynamic_slice.59
  682.6 0.2 iota_compare_fusion.2
  682.8 4.9 constant_dynamic-slice_fusion.4
  687.8 74.1 %fusion.97 = (f32[8,16,128]{2,1,0:T(8,128)S(1)}, f32[8,16,128,2048]{3,2,1,0:T(8,128)}) fusion(pred[128,2048]{1,0:T(8,128)(4,1)S(1)} %iota_compare_fusion.2, bf16[8,2048,16,128]{3,1,2,0:T(8,128)(2,1)} %get-tuple-element.206, bf16[8,128,16,128]{3,2,1,0:T(8,128)(2,1)} %constant_dynamic-slice_fusion.4), kind=kOutput, calls=%fused_computation.118.clone.1 | convolution fusion | flops 8724154368 | bytes 205848576 | tf_op jit(solution)/shard_map/while/body/eval_jaxpr/sub | solution.py:44
  761.9 63.0 %bitcast_dynamic-update-slice_fusion.2 = bf16[2,8,128,16,128]{4,2,3,1,0:T(8,128)(2,1)} fusion(bf16[2,8,128,16,128]{4,2,3,1,0:T(8,128)(2,1)} %get-tuple-element.191, s32[]{:T(128)S(6)} %copy.90, bf16[8,2048,16,128]{3,1,2,0:T(8,128)(2,1)} %get-tuple-element.207, f32[8,16,128,2048]{3,2,1,0:T(8,128)} %get-tuple-element.177, ...), kind=kOutput, calls=%fused_computation.11.clone.2 | convolution fusion | flops 8659140608 | bytes 205586432 | tf_op jit(solution)/shard_map/while/body/eval_jaxpr/bhqk,bkhd->bqhd/dot_general | solution.py:45
  824.9 0.6 dynamic_slice.59
  826.2 0.2 iota_compare_fusion.2
  826.4 4.9 constant_dynamic-slice_fusion.4
  831.3 74.1 %fusion.97 = (f32[8,16,128]{2,1,0:T(8,128)S(1)}, f32[8,16,128,2048]{3,2,1,0:T(8,128)}) fusion(pred[128,2048]{1,0:T(8,128)(4,1)S(1)} %iota_compare_fusion.2, bf16[8,2048,16,128]{3,1,2,0:T(8,128)(2,1)} %get-tuple-element.206, bf16[8,128,16,128]{3,2,1,0:T(8,128)(2,1)} %constant_dynamic-slice_fusion.4), kind=kOutput, calls=%fused_computation.118.clone.1 | convolution fusion | flops 8724154368 | bytes 205848576 | tf_op jit(solution)/shard_map/while/body/eval_jaxpr/sub | solution.py:44
  905.4 63.0 %bitcast_dynamic-update-slice_fusion.2 = bf16[2,8,128,16,128]{4,2,3,1,0:T(8,128)(2,1)} fusion(bf16[2,8,128,16,128]{4,2,3,1,0:T(8,128)(2,1)} %get-tuple-element.191, s32[]{:T(128)S(6)} %copy.90, bf16[8,2048,16,128]{3,1,2,0:T(8,128)(2,1)} %get-tuple-element.207, f32[8,16,128,2048]{3,2,1,0:T(8,128)} %get-tuple-element.177, ...), kind=kOutput, calls=%fused_computation.11.clone.2 | convolution fusion | flops 8659140608 | bytes 205586432 | tf_op jit(solution)/shard_map/while/body/eval_jaxpr/bhqk,bkhd->bqhd/dot_general | solution.py:45
  968.6 13.9 %copy.31 = bf16[8,2,128,16,128]{4,3,2,1,0:T(8,128)(2,1)} copy(bf16[8,2,128,16,128]{4,2,3,0,1:T(8,128)(2,1)} %bitcast.118) | data formatting | bytes 16777216 | tf_op jit(solution)/shard_map/transpose | solution.py:48
  982.5 13.3 %reshape.259 = bf16[8,256,2048]{2,1,0:T(8,128)(2,1)} reshape(bf16[8,2,128,16,128]{4,3,2,1,0:T(8,128)(2,1)} %copy.31) | data formatting | bytes 16777216 | tf_op jit(solution)/shard_map/reshape | solution.py:48
  995.8 11.5 %constant_dynamic-slice_fusion.2 = bf16[8,2048,2,128]{3,2,1,0:T(2,128)(2,1)S(1)} fusion(bf16[8,2048,16,128]{3,2,1,0:T(8,128)(2,1)} %all-gather.4.cloned.1.call-done, s32[]{:T(128)S(6)} %select_n.11), kind=kLoop, calls=%fused_computation.106 | loop fusion | bytes 16777220 | tf_op jit(solution)/shard_map/dynamic_slice | solution.py:70
  1007.3 20.6 %pad_maximum_fusion = bf16[8,2049,2,128]{3,2,1,0:T(2,128)(2,1)S(1)} fusion(bf16[8,1,2,128]{3,2,1,0:T(2,128)(2,1)S(1)} %copy-done.7, bf16[8,2048,2,128]{3,2,1,0:T(2,128)(2,1)S(1)} %constant_dynamic-slice_fusion.2), kind=kLoop, calls=%fused_computation.40 | loop fusion | flops 4196352 | bytes 16785408 | tf_op jit(solution)/shard_map/concatenate | solution.py:83
  1027.9 0.0 copy-start
  1027.9 3.4 copy-done
  1031.3 2.3 fusion.27
  1033.6 0.2 fusion.44
  1033.8 11.7 %constant_dynamic-slice_fusion.1 = bf16[8,2048,2,128]{3,2,1,0:T(2,128)(2,1)S(1)} fusion(bf16[8,2048,16,128]{3,2,1,0:T(8,128)(2,1)} %all-gather.6.cloned.1.call-done, s32[]{:T(128)S(6)} %select_n.11), kind=kLoop, calls=%fused_computation.103 | loop fusion | bytes 16777220 | tf_op jit(solution)/shard_map/dynamic_slice | solution.py:71
  1045.5 20.6 %pad_maximum_fusion.1 = bf16[8,2049,2,128]{3,2,1,0:T(2,128)(2,1)S(1)} fusion(bf16[8,1,2,128]{3,2,1,0:T(2,128)(2,1)S(1)} %copy-done.6, bf16[8,2048,2,128]{3,2,1,0:T(2,128)(2,1)S(1)} %constant_dynamic-slice_fusion.1), kind=kLoop, calls=%fused_computation.41 | loop fusion | flops 4196352 | bytes 16785408 | tf_op jit(solution)/shard_map/concatenate | solution.py:84
  1066.2 1.8 fusion.25
  1068.0 2.3 convolution_convert_fusion
  1070.3 13.1 %all-gather = bf16[64,2048]{1,0:T(8,128)(2,1)S(1)} all-gather(bf16[8,2048]{1,0:T(8,128)(2,1)S(1)} %convolution_convert_fusion), channel_id=2, replica_groups=mesh['dp'=4,'sp'=8] {'sp'}, dimensions={0}, use_global_device_ids=true | all-gather | bytes 294912 | tf_op jit(solution)/shard_map/all_gather | solution.py:89
  1083.4 0.1 multiply_reduce_fusion.3
  1083.6 0.0 copy-start.5
  1083.6 21.8 %multiply_reduce_fusion = (f32[8,256]{1,0:T(8,128)S(1)}, f32[8,256,2048]{2,1,0:T(8,128)S(1)}) fusion(bf16[8,256,2048]{2,1,0:T(8,128)(2,1)} %reshape.259, bf16[2048,2048]{1,0:T(8,128)(2,1)} %param.15), kind=kOutput, calls=%fused_computation.31 | convolution fusion | flops 17188255744 | bytes 33562624 | tf_op jit(solution)/shard_map/dot_general | solution.py:68
  1105.5 0.7 add_convert_fusion.1
  1106.2 8.2 add_convert_fusion
  (40 shorter events, 0.2 us)
Async XLA Ops:
  7.2 332.6 %all-gather.6.cloned.1.call-start = ((), (), s32[]{:S(2)}) async-start(), calls=%async_computation.1 | async-start | bytes 75497472 | tf_op jit(solution)/shard_map/all_gather | solution.py:66
  40.7 596.0 %all-gather.4.cloned.1.call-start = ((), (), s32[]{:S(2)}) async-start(), calls=%async_computation | async-start | bytes 75497472 | tf_op jit(solution)/shard_map/all_gather | solution.py:65
  41.2 21.9 %copy-start.8 = (f32[2048]{0:T(1024)S(1)}, f32[2048]{0:T(1024)}, u32[]{:S(2)}) copy-start(f32[2048]{0:T(1024)} %param.16) | copy-start | bytes 24580
  72.1 21.8 %copy-start.9 = (f32[2048]{0:T(1024)S(1)}, f32[2048]{0:T(1024)}, u32[]{:S(2)}) copy-start(f32[2048]{0:T(1024)} %param.17) | copy-start | bytes 24580
  149.3 39.5 %copy-start.2 = (bf16[8,2048]{1,0:T(8,128)(2,1)S(1)}, bf16[8,2048]{1,0:T(8,128)(2,1)}, u32[]{:S(2)}) copy-start(bf16[8,2048]{1,0:T(8,128)(2,1)} %param.19) | copy-start | bytes 98308
  681.3 1.3 copy-start.10
  761.9 63.0 %copy-start.11 = (s32[2]{0:T(128)S(1)}, s32[2]{0:T(128)}, u32[]{:S(2)}) copy-start(s32[2]{0:T(128)} %copy-done.10) | copy-start | bytes 28 | tf_op jit(solution)/shard_map/while
  824.9 1.3 copy-start.10
  905.4 63.0 %copy-start.11 = (s32[2]{0:T(128)S(1)}, s32[2]{0:T(128)}, u32[]{:S(2)}) copy-start(s32[2]{0:T(128)} %copy-done.10) | copy-start | bytes 28 | tf_op jit(solution)/shard_map/while
  982.5 24.8 %copy-start.7 = (bf16[8,1,2,128]{3,2,1,0:T(2,128)(2,1)S(1)}, bf16[8,1,2,128]{3,2,1,0:T(2,128)(2,1)}, u32[]{:S(2)}) copy-start(bf16[8,1,2,128]{3,2,1,0:T(2,128)(2,1)} %fusion.58) | copy-start | bytes 12292
  995.8 35.5 %copy-start.4 = (bf16[8,2,128,1]{2,0,1,3:T(8,128)(2,1)S(1)}, bf16[8,2,128,1]{2,0,1,3:T(8,128)(2,1)}, u32[]{:S(2)}) copy-start(bf16[8,2,128,1]{2,0,1,3:T(8,128)(2,1)} %fusion.64) | copy-start | bytes 12292
  1027.9 3.4 copy-start
  1031.3 14.3 %copy-start.6 = (bf16[8,1,2,128]{3,2,1,0:T(2,128)(2,1)S(1)}, bf16[8,1,2,128]{3,2,1,0:T(2,128)(2,1)}, u32[]{:S(2)}) copy-start(bf16[8,1,2,128]{3,2,1,0:T(2,128)(2,1)} %copy.35) | copy-start | bytes 12292
  1066.2 39.3 %copy-start.1 = (bf16[8,2049,2,128]{3,2,1,0:T(2,128)(2,1)}, bf16[8,2049,2,128]{3,2,1,0:T(2,128)(2,1)S(1)}, u32[]{:S(2)}) copy-start(bf16[8,2049,2,128]{3,2,1,0:T(2,128)(2,1)S(1)} %pad_maximum_fusion.1) | copy-start | bytes 25178116
  1083.6 21.9 %copy-start.3 = (bf16[8,2048]{1,0:T(8,128)(2,1)S(1)}, bf16[8,2048]{1,0:T(8,128)(2,1)}, u32[]{:S(2)}) copy-start(bf16[8,2048]{1,0:T(8,128)(2,1)} %param.19) | copy-start | bytes 98308
  1083.6 21.9 %copy-start.5 = (f32[2048]{0:T(1024)S(1)}, f32[2048]{0:T(1024)}, u32[]{:S(2)}) copy-start(f32[2048]{0:T(1024)} %param.18) | copy-start | bytes 24580
Sparse Core Ops, SparseCore 0:
  40.8 298.9 all-gather.5
  342.0 294.6 all-gather.3
where the time goes:
time: 1130 us; the launch traced here: 1120 us
  waiting for transfers between devices  382 us (34%)
  matrix products  374 us (33%)
  local copies, waits for them, and re-layouts  179 us (16%)
  other arithmetic  142 us (13%)
  blocking collectives  27.6 us (2%)
  between operations  14.8 us (1%)
    all_gather x1, waiting for transfers between devices, device_step(): k_all = lax.all_gather(k_loc, 'sp', axis=1, tiled=True)  252 us
    sub x2, matrix products, one_block(): attn_p = jax.nn.softmax(scores, axis=-1).astype(jnp.bfloat16)  148 us
    all_gather x1, waiting for transfers between devices, device_step(): v_all = lax.all_gather(v_loc, 'sp', axis=1, tiled=True)  129 us
    dot_general x2, matrix products, one_block(): jnp.einsum('bhqk,bkhd->bqhd', attn_p, v_all, preferred_element_type=jnp.f...  126 us
    unnamed x25, local copies, waits for them, and re-layouts  117 us
    neg x3, other arithmetic, apply_rope(): -values[..., half_dim:]  45.8 us
    dot_general x2, matrix products, project_heads(): jnp.dot(x_rows, w_mat, preferred_element_type=jnp.float32)  43.7 us
    convert_element_type x1, other arithmetic, project_heads(): apply_rope(normed.reshape(x_rows.shape[:-1] + (-1, HEAD_DIM)), cos_t, sin_t)  39.3 us
  transfers between devices with their start and end apart: 2, of which 2 were waited for; matrix products, arithmetic and copies ran while one was open for 18% of the time, Pallas kernels for 0%

commit v1 on v0

v1 whole, which is shorter than its diff:
```python
import functools

import jax
import jax.numpy as jnp
from jax import lax
from jax.experimental import pallas as pl
from jax.experimental.pallas import tpu as pltpu
from jax.sharding import PartitionSpec as P

HEAD_DIM = 128
ROPE_THETA = 500000.0
NORM_EPS = 1e-6
CORES = 2
LOG2E = 1.4426950408889634
SLOTS = 3
COL_TILE = 512
VMEM_BYTES = 66_000_000


def rope_tables(positions):
    inv_freq = ROPE_THETA ** (-jnp.arange(0, HEAD_DIM, 2).astype(jnp.float32) / HEAD_DIM)
    angles = positions.astype(jnp.float32)[:, None] * inv_freq[None, :]
    cos_t, sin_t = jnp.cos(angles), jnp.sin(angles)
    return jnp.concatenate([cos_t, cos_t], axis=-1), jnp.concatenate([-sin_t, sin_t], axis=-1)


def rotate(values, cos_t, sin_t):
    return values * cos_t + pltpu.roll(values, HEAD_DIM // 2, 1) * sin_t


def exchange_kernel(group_n, x_hbm, wq_hbm, wk_hbm, wv_hbm, wo_hbm, gains_ref, post_ref, cos_ref, sin_ref, cosd_ref, sind_ref, new_ref,
                    qkv_ref, o_ref, rel_ref, relo_ref, knew_ref, vnew_ref, outd_ref,
                    w_vm, x_vm, raw_vm, ssq_vm, stage_vm, qkv_vm, ostage_vm, wo_vm, qnew_vm, deco_vm, decp_vm,
                    w_sem, x_sem, wo_sem, send_sem, recv_sem, rel_sem, fwd_sem, load_sem, osend_sem, orecv_sem, relo_sem, decs_sem, decr_sem):
    n_batch, tok, width = x_hbm.shape
    cols = width // group_n
    heads = cols // HEAD_DIM
    seq = tok * group_n
    half = tok // 2
    chips = group_n // CORES
    me = lax.axis_index("sp")
    chip, core = me // CORES, me % CORES
    right = (chip + 1) % chips
    left = (chip + chips - 1) % chips
    far = (chip + 2) % chips
    right_dev, left_dev = right * CORES + core, left * CORES + core
    partner = chip * CORES + (1 - core)
    w_hbm = (wq_hbm, wk_hbm, wv_hbm)
    scale2 = HEAD_DIM ** -0.5 * LOG2E

    def remote(src, dst, s_sem, r_sem, dev):
        return pltpu.make_async_remote_copy(src_ref=src, dst_ref=dst, send_sem=s_sem, recv_sem=r_sem,
                                            device_id={"sp": dev}, device_id_type=pl.DeviceIdType.MESH)

    def drain(ref, sem):
        pltpu.make_async_copy(ref, ref, sem).wait()

    def w_copy(j):
        return pltpu.make_async_copy(w_hbm[j], w_vm.at[j], w_sem.at[j])

    def x_copy(t):
        return pltpu.make_async_copy(x_hbm.at[t], x_vm.at[lax.rem(t, 2)], x_sem.at[lax.rem(t, 2)])

    x_copy(0).start()
    for j in range(3):
        w_copy(j).start()
    wo_copy = pltpu.make_async_copy(wo_hbm.at[pl.ds(me * cols, cols)], wo_vm, wo_sem)
    wo_copy.start()

    barrier = pltpu.get_barrier_semaphore()
    for step in range(1, group_n):
        pl.semaphore_signal(barrier, inc=1, device_id={"sp": lax.rem(me + step, group_n)}, device_id_type=pl.DeviceIdType.MESH)
    pl.semaphore_wait(barrier, group_n - 1)

    def send_tensor(t, slot, j):
        rows = pl.ds(me * tok, tok)
        far_devs = pl.ds(far * CORES, CORES)
        remote(stage_vm.at[slot, j, far_devs, pl.ds(0, half)], rel_ref.at[t, 0, :, j], send_sem.at[t], rel_sem.at[t], right_dev).start()
        remote(stage_vm.at[slot, j, far_devs, pl.ds(half, half)], rel_ref.at[t, 1, :, j], send_sem.at[t], rel_sem.at[t], left_dev).start()
        for side in (right, left):
            for c in range(CORES):
                dev = side * CORES + c
                remote(stage_vm.at[slot, j, dev], qkv_ref.at[j, t, rows], send_sem.at[t], recv_sem.at[t], dev).start()
        remote(stage_vm.at[slot, j, partner], qkv_ref.at[j, t, rows], send_sem.at[t], recv_sem.at[t], partner).start()
        pltpu.make_async_copy(stage_vm.at[slot, j, me], qkv_ref.at[j, t, rows], recv_sem.at[t]).start()

    def drain_sends(t):
        drain(stage_vm.at[lax.rem(t, SLOTS), :, pl.ds(0, group_n - 1)], send_sem.at[t])

    def project(t):
        slot = lax.rem(t, SLOTS)

        @pl.when(t >= SLOTS)
        def _():
            drain_sends(t - SLOTS)

        x_copy(t).wait()

        @pl.when(t + 1 < n_batch)
        def _():
            x_copy(t + 1).start()

        x_slot = lax.rem(t, 2)
        for j in range(3):
            @pl.when(t == 0)
            def _():
                w_copy(j).wait()

            ssq_vm[...] = jnp.zeros_like(ssq_vm)

            def col_tile(n, _):
                at = pl.ds(pl.multiple_of(n * COL_TILE, COL_TILE), COL_TILE)
                acc = jnp.dot(x_vm[x_slot], w_vm[j, :, at], preferred_element_type=jnp.float32)
                if j < 2:
                    raw_vm[:, at] = acc
                    sq = acc * acc
                    ssq_vm[...] += sum(sq[:, i * HEAD_DIM:(i + 1) * HEAD_DIM] for i in range(COL_TILE // HEAD_DIM))
                else:
                    for i in range(COL_TILE // cols):
                        stage_vm[slot, j, n * (COL_TILE // cols) + i] = acc[:, i * cols:(i + 1) * cols].astype(jnp.bfloat16)
                return 0

            lax.fori_loop(0, width // COL_TILE, col_tile, 0)
            if j < 2:
                inv = lax.rsqrt(jnp.sum(ssq_vm[...], axis=1, keepdims=True) / width + NORM_EPS)

                def group_tile(n, _):
                    for h in range(heads):
                        at = pl.ds(pl.multiple_of(n * cols + h * HEAD_DIM, HEAD_DIM), HEAD_DIM)
                        normed = raw_vm[:, at] * inv * gains_ref[j:j + 1, at]
                        stage_vm[slot, j, n, :, h * HEAD_DIM:(h + 1) * HEAD_DIM] = rotate(normed, cos_ref[...], sin_ref[...]).astype(jnp.bfloat16)
                    return 0

                lax.fori_loop(0, group_n, group_tile, 0)
            send_tensor(t, slot, j)

    def forward(b):
        drain(rel_ref.at[b], rel_sem.at[b])
        for way, came, to, first in ((0, left_dev, right, 0), (1, right_dev, left, half)):
            for c in range(CORES):
                remote(rel_ref.at[b, way, c], qkv_ref.at[:, b, pl.ds(came * tok + first, half)], fwd_sem.at[0], recv_sem.at[b], to * CORES + c).start()

    def forward_o(b):
        drain(relo_ref.at[b], relo_sem.at[b])
        for way, came, to, first in ((0, left_dev, right, 0), (1, right_dev, left, half)):
            for c in range(CORES):
                remote(relo_ref.at[b, way, c], o_ref.at[b, came, pl.ds(first, half)], fwd_sem.at[1], orecv_sem.at[b], to * CORES + c).start()

    def send_o(b, slot, dev):
        src = ostage_vm.at[slot, pl.ds(dev * tok, tok)]
        away = lax.rem(dev // CORES - chip + chips, chips)

        @pl.when(dev == me)
        def _():
            pltpu.make_async_copy(src, o_ref.at[b, me], osend_sem.at[b]).start()

        @pl.when(jnp.logical_and(dev != me, away != 2))
        def _():
            remote(src, o_ref.at[b, me], osend_sem.at[b], orecv_sem.at[b], dev).start()

        @pl.when(away == 2)
        def _():
            c = dev % CORES
            remote(ostage_vm.at[slot, pl.ds(dev * tok, half)], relo_ref.at[b, 0, c], osend_sem.at[b], relo_sem.at[b], right_dev).start()
            remote(ostage_vm.at[slot, pl.ds(dev * tok + half, half)], relo_ref.at[b, 1, c], osend_sem.at[b], relo_sem.at[b], left_dev).start()

    def new_row():
        def full(j):
            def col_tile(n, ssq):
                at = pl.ds(pl.multiple_of(n * COL_TILE, COL_TILE), COL_TILE)
                acc = jnp.dot(new_ref[...], w_vm[j, :, at], preferred_element_type=jnp.float32)
                return ssq + jnp.sum(acc * acc, axis=1, keepdims=True)

            ssq = lax.fori_loop(0, width // COL_TILE, col_tile, jnp.zeros((n_batch, 1), jnp.float32))
            return lax.rsqrt(ssq / width + NORM_EPS)

        own = pl.ds(pl.multiple_of(me * cols, cols), cols)
        for j, to in ((0, qnew_vm), (1, knew_ref)):
            inv = full(j)
            raw = jnp.dot(new_ref[...], w_vm[j, :, own], preferred_element_type=jnp.float32)
            normed = raw * inv * gains_ref[j:j + 1, own]
            for h in range(heads):
                at = slice(h * HEAD_DIM, (h + 1) * HEAD_DIM)
                to[:, at] = rotate(normed[:, at], cosd_ref[...], sind_ref[...]).astype(jnp.bfloat16)
        vnew_ref[...] = jnp.dot(new_ref[...], w_vm[2, :, own], preferred_element_type=jnp.float32).astype(jnp.bfloat16)
        deco_vm[...] = jnp.zeros_like(deco_vm)

    def attend(b):
        slot = lax.rem(b, 2)
        drain(qkv_ref.at[:, b], recv_sem.at[b])
        load = pltpu.make_async_copy(qkv_ref.at[:, b], qkv_vm, load_sem)
        load.start()

        @pl.when(b >= 2)
        def _():
            drain(ostage_vm.at[slot], osend_sem.at[b - 2])

        load.wait()
        keep = lax.broadcasted_iota(jnp.int32, (tok, tok), 0) >= lax.broadcasted_iota(jnp.int32, (tok, tok), 1)
        contract_last = (((1,), (1,)), ((), ()))
        for blk in range(group_n):
            rows = slice(blk * tok, (blk + 1) * tok)

            def one_head(h, _):
                at = pl.ds(pl.multiple_of(h * HEAD_DIM, HEAD_DIM), HEAD_DIM)
                q = qkv_vm[0, rows, at]
                diag = lax.dot_general(q, qkv_vm[1, rows, at], contract_last, preferred_element_type=jnp.float32)
                diag = jnp.where(keep, diag, -jnp.inf)
                top = jnp.max(diag, axis=1, keepdims=True)
                if blk:
                    past = lax.dot_general(q, qkv_vm[1, :blk * tok, at], contract_last, preferred_element_type=jnp.float32)
                    top = jnp.maximum(top, jnp.max(past, axis=1, keepdims=True))
                    past = jnp.exp2((past - top) * scale2)
                diag = jnp.exp2((diag - top) * scale2)
                total = jnp.sum(diag, axis=1, keepdims=True)
                if blk:
                    total = total + jnp.sum(past, axis=1, keepdims=True)
                inv = 1.0 / total
                out = jnp.dot((diag * inv).astype(jnp.bfloat16), qkv_vm[2, rows, at], preferred_element_type=jnp.float32)
                if blk:
                    out = out + jnp.dot((past * inv).astype(jnp.bfloat16), qkv_vm[2, :blk * tok, at], preferred_element_type=jnp.float32)
                ostage_vm[slot, rows, at] = out.astype(jnp.bfloat16)
                return 0

            lax.fori_loop(0, heads, one_head, 0)
            send_o(b, slot, blk)

        mine = lax.broadcasted_iota(jnp.int32, (n_batch, HEAD_DIM), 0) == b
        for h in range(heads):
            at = slice(h * HEAD_DIM, (h + 1) * HEAD_DIM)
            q = qnew_vm[:, at]
            past = lax.dot_general(q, qkv_vm[1, :, at], contract_last, preferred_element_type=jnp.float32)
            last = jnp.sum(q.astype(jnp.float32) * knew_ref[:, at].astype(jnp.float32), axis=1, keepdims=True)
            top = jnp.maximum(jnp.max(past, axis=1, keepdims=True), last)
            past, last = jnp.exp2((past - top) * scale2), jnp.exp2((last - top) * scale2)
            inv = 1.0 / (jnp.sum(past, axis=1, keepdims=True) + last)
            out = jnp.dot((past * inv).astype(jnp.bfloat16), qkv_vm[2, :, at], preferred_element_type=jnp.float32)
            out = out + (last * inv).astype(jnp.bfloat16).astype(jnp.float32) * vnew_ref[:, at].astype(jnp.float32)
            deco_vm[:, at] = jnp.where(mine, out, deco_vm[:, at])

    def send_part():
        wo_copy.wait()
        part = jnp.dot(deco_vm[...].astype(jnp.bfloat16), wo_vm[...], preferred_element_type=jnp.float32)
        decp_vm[me] = part.astype(jnp.bfloat16)
        for step in range(1, group_n):
            remote(decp_vm.at[me], decp_vm.at[me], decs_sem, decr_sem, lax.rem(me + step, group_n)).start()

    def step(t, _):
        @pl.when(t < n_batch)
        def _():
            project(t)

        @pl.when(t == 1)
        def _():
            new_row()

        @pl.when(jnp.logical_and(t >= 1, t <= n_batch))
        def _():
            forward(t - 1)

        @pl.when(t >= 3)
        def _():
            forward_o(t - 3)

        @pl.when(jnp.logical_and(t >= 2, t <= n_batch + 1))
        def _():
            attend(t - 2)

        return 0

    lax.fori_loop(0, n_batch + 2, step, 0)
    send_part()
    forward_o(n_batch - 1)

    drain(decp_vm.at[pl.ds(0, group_n - 1)], decs_sem)
    drain(decp_vm.at[pl.ds(0, group_n - 1)], decr_sem)
    proj = decp_vm[0].astype(jnp.float32)
    for g in range(1, group_n):
        proj = proj + decp_vm[g].astype(jnp.float32)
    inv = lax.rsqrt(jnp.sum(proj * proj, axis=1, keepdims=True) / width + NORM_EPS)
    outd_ref[...] = (new_ref[...].astype(jnp.float32) + proj * inv * post_ref[...]).astype(jnp.bfloat16)

    for t in range(n_batch - SLOTS, n_batch):
        drain_sends(t)
    for b in range(n_batch - 2, n_batch):
        drain(ostage_vm.at[b % 2], osend_sem.at[b])
    drain(rel_ref, fwd_sem.at[0])
    drain(relo_ref, fwd_sem.at[1])
    for b in range(n_batch):
        drain(o_ref.at[b, pl.ds(0, group_n - 1)], orecv_sem.at[b])


def output_kernel(o_ref, x_ref, wo_ref, post_ref, k_ref, v_ref, knew_ref, vnew_ref, out_ref, kc_ref, vc_ref, raw_vm):
    group_n, tok, cols = o_ref.shape[1:]
    width = group_n * cols
    heads = cols // HEAD_DIM
    o_all = jnp.concatenate([o_ref[0, g] for g in range(group_n)], axis=1)
    ssq = jnp.zeros((tok, 1), jnp.float32)
    for n in range(width // COL_TILE):
        at = slice(n * COL_TILE, (n + 1) * COL_TILE)
        acc = jnp.dot(o_all, wo_ref[:, at], preferred_element_type=jnp.float32)
        raw_vm[:, at] = acc
        ssq = ssq + jnp.sum(acc * acc, axis=1, keepdims=True)
    inv = lax.rsqrt(ssq / width + NORM_EPS)
    out_ref[0] = (x_ref[0].astype(jnp.float32) + raw_vm[...] * inv * post_ref[...]).astype(jnp.bfloat16)
    seq = k_ref.shape[2]
    for src, new, to in ((k_ref, knew_ref, kc_ref), (v_ref, vnew_ref, vc_ref)):
        to[0, :seq] = src[0, 0].reshape(seq, heads, HEAD_DIM)
        to[0, seq:] = new[0].reshape(1, heads, HEAD_DIM)


def solution(mesh):
    group_n = mesh.shape["sp"]

    def device_step(prompt_blk, w_q, w_k, w_v, w_o, q_norm_w, k_norm_w, post_norm_w, new_rows):
        n_batch, tok, width = prompt_blk.shape
        cols = width // group_n
        heads = cols // HEAD_DIM
        seq = tok * group_n
        half = tok // 2
        bf16, f32 = jnp.bfloat16, jnp.float32
        cos_p, sin_p = rope_tables(lax.axis_index("sp") * tok + jnp.arange(tok))
        cos_d, sin_d = rope_tables(jnp.full((1,), seq))
        gains = jnp.stack([q_norm_w, k_norm_w])
        post = post_norm_w[None]
        any_spec = pl.BlockSpec(memory_space=pl.ANY)
        vm_spec = pl.BlockSpec(memory_space=pltpu.VMEM)
        dma = pltpu.SemaphoreType.DMA
        qkv, o_all, _, _, k_new, v_new, out_d = pl.pallas_call(
            functools.partial(exchange_kernel, group_n),
            out_shape=(
                jax.ShapeDtypeStruct((3, n_batch, seq, cols), bf16),
                jax.ShapeDtypeStruct((n_batch, group_n, tok, cols), bf16),
                jax.ShapeDtypeStruct((n_batch, 2, CORES, 3, half, cols), bf16),
                jax.ShapeDtypeStruct((n_batch, 2, CORES, half, cols), bf16),
                jax.ShapeDtypeStruct((n_batch, cols), bf16),
                jax.ShapeDtypeStruct((n_batch, cols), bf16),
                jax.ShapeDtypeStruct((n_batch, width), bf16),
            ),
            in_specs=[any_spec] * 5 + [vm_spec] * 7,
            out_specs=(any_spec,) * 4 + (vm_spec,) * 3,
            scratch_shapes=[
                pltpu.VMEM((3, width, width), bf16),
                pltpu.VMEM((2, tok, width), bf16),
                pltpu.VMEM((tok, width), f32),
                pltpu.VMEM((tok, HEAD_DIM), f32),
                pltpu.VMEM((SLOTS, 3, group_n, tok, cols), bf16),
                pltpu.VMEM((3, seq, cols), bf16),
                pltpu.VMEM((2, seq, cols), bf16),
                pltpu.VMEM((cols, width), bf16),
                pltpu.VMEM((n_batch, cols), bf16),
                pltpu.VMEM((n_batch, cols), f32),
                pltpu.VMEM((group_n, n_batch, width), bf16),
                dma((3,)), dma((2,)), dma,
                dma((n_batch,)), dma((n_batch,)), dma((n_batch,)), dma((2,)), dma,
                dma((n_batch,)), dma((n_batch,)), dma((n_batch,)), dma, dma,
            ],
            compiler_params=pltpu.CompilerParams(collective_id=0, has_side_effects=True, vmem_limit_bytes=VMEM_BYTES),
        )(prompt_blk, w_q, w_k, w_v, w_o, gains, post, cos_p, sin_p, cos_d, sin_d, new_rows)

        row = lambda shape, at: pl.BlockSpec((1,) + shape, lambda b: (b,) + at)
        out_p, k_cache, v_cache = pl.pallas_call(
            output_kernel,
            grid=(n_batch,),
            out_shape=(
                jax.ShapeDtypeStruct((n_batch, tok, width), bf16),
                jax.ShapeDtypeStruct((n_batch, seq + 1, heads, HEAD_DIM), bf16),
                jax.ShapeDtypeStruct((n_batch, seq + 1, heads, HEAD_DIM), bf16),
            ),
            in_specs=[
                row((group_n, tok, cols), (0, 0, 0)),
                row((tok, width), (0, 0)),
                vm_spec,
                vm_spec,
                pl.BlockSpec((1, 1, seq, cols), lambda b: (1, b, 0, 0)),
                pl.BlockSpec((1, 1, seq, cols), lambda b: (2, b, 0, 0)),
                row((1, cols), (0, 0)),
                row((1, cols), (0, 0)),
            ],
            out_specs=(row((tok, width), (0, 0)), row((seq + 1, heads, HEAD_DIM), (0, 0, 0)), row((seq + 1, heads, HEAD_DIM), (0, 0, 0))),
            scratch_shapes=[pltpu.VMEM((tok, width), f32)],
            compiler_params=pltpu.CompilerParams(vmem_limit_bytes=VMEM_BYTES),
        )(o_all, prompt_blk, w_o, post, qkv, qkv, k_new[:, None], v_new[:, None])
        return out_p, k_cache, v_cache, out_d

    replicated = P()
    return jax.shard_map(
        device_step, mesh=mesh,
        in_specs=(P("dp", "sp", None), replicated, replicated, replicated, replicated, replicated, replicated, replicated, P("dp", None)),
        out_specs=(P("dp", "sp", None), P("dp", None, "sp", None), P("dp", None, "sp", None), P("dp", None)),
        check_vma=False)
```

time: 1130 us -> 428 us (0.38)
  Pallas kernels: 0 us -> 419 us
  waiting for transfers between devices: 382 us -> 0 us
  matrix products: 374 us -> 0 us
  local copies, waits for them, and re-layouts: 179 us -> 3.18 us
  other arithmetic: 142 us -> 4.01 us
  blocking collectives: 27.6 us -> 0 us
  between operations: 14.8 us -> 0.68 us
    pallas_call x0 -> x2, Pallas kernels: none -> 419 us  [the longest x1 387 us: device_step(): pl.pallas_call(functools.partial(exchange_kernel, group_n), out_shape=(ja...]
    all_gather x2 -> x0, waiting for transfers between devices: 382 us -> none  [the longest x1 252 us: device_step(): k_all = lax.all_gather(k_loc, 'sp', axis=1, tiled=True)]
    dot_general x12 -> x0, matrix products: 226 us -> none  [the longest x2 126 us: one_block(): jnp.einsum('bhqk,bkhd->bqhd', attn_p, v_all, preferred_element_type=jnp.f...]
    sub x2 -> x0, matrix products: 148 us -> none  [one_block(): attn_p = jax.nn.softmax(scores, axis=-1).astype(jnp.bfloat16)]
    unnamed x25 -> x3, local copies, waits for them, and re-layouts: 117 us -> 0.62 us
    convert_element_type x5 -> x0, other arithmetic: 49.5 us -> none  [the longest x1 39.3 us: project_heads(): apply_rope(normed.reshape(x_rows.shape[:-1] + (-1, HEAD_DIM)), cos_t, sin_t)]
    neg x3 -> x1, other arithmetic: 45.8 us -> 0.53 us  [rope_tables(): -sin_t]
    concatenate x2 -> x3, other arithmetic: 41.2 us -> 2.03 us  [the longest x2 1.43 us: rope_tables(): jnp.concatenate([cos_t, cos_t], axis=-1)]
  transfers between devices with their start and end apart: 2 -> 0, of which waited for: 2 -> 0; matrix products, arithmetic and copies ran while one was open for 18% -> 0% of each run, Pallas kernels for 0% -> 0%
where the time goes in v1:
time: 428 us; the launch traced here: 427 us
  Pallas kernels  419 us (98%)
    pallas_call x1, Pallas kernels, device_step(): pl.pallas_call(functools.partial(exchange_kernel, group_n), out_shape=(ja...  387 us
    pallas_call x1, Pallas kernels, device_step(): pl.pallas_call(output_kernel, grid=(n_batch,), out_shape=(jax.ShapeDtypeS...  31.8 us

profile of v1, /device:TPU:81, one launch (start us, length us, event | category | flops | bytes accessed | tf_op | source)
XLA Modules:
  0.0 427.1 jit_solution(14155843992455419684)
XLA Ops:
  0.7 0.6 pad_maximum_fusion.3.cosd_ref
  1.3 0.1 fusion.1
  1.4 0.6 pad_maximum_fusion.4.sind_ref
  2.0 1.3 pad_maximum_fusion.2.gains_ref
  3.3 0.5 fusion
  3.8 0.8 pad_maximum_fusion
  4.7 387.4 %shard_map.120 = (bf16[3,8,2048,256]{3,2,1,0:T(8,128)(2,1)}, bf16[8,8,256,256]{3,2,1,0:T(8,128)(2,1)}, bf16[8,2,2,3,128,256]{5,4,3,2,1,0:T(8,128)(2,1)}, bf16[8,...) custom-call(bf16[8,256,2048]{2,1,0:T(8,128)(2,1)} %x_ref.1, ...), custom_call_target="tpu_custom_call" | custom-call | tf_op jit(solution)/shard_map/pallas_call | solution.py:329
  392.1 1.3 copy.13.knew_ref
  393.4 1.3 copy.14.vnew_ref
  394.7 0.0 copy-start
  394.7 31.8 %shard_map.121 = (bf16[8,256,2048]{2,1,0:T(8,128)(2,1)}, bf16[8,2049,2,128]{3,2,1,0:T(2,128)(2,1)}, bf16[8,2049,2,128]{3,2,1,0:T(2,128)(2,1)}) custom-call(bf16[8,8,256,256]{3,2,1,0:T(8,128)(2,1)} %get-tuple-element.12.o_ref, bf16[8,256,2048]{2,1,0:T(8,128)(2,1)} %x_ref.1, bf16[2048,2048]{1,0:T(8,128)(2,1)} %wo_ref.1, f32[1,2048]{1,0:T(1,128)} %bitcast.6, ...), custom_call_target="tpu_custom_call" | custom-call | tf_op jit(solution)/shard_map/pallas_call | solution.py:362
  426.5 0.0 copy-done
  426.5 0.6 copy.16
  (3 shorter events, 0.1 us)
Async XLA Ops:
  394.7 31.8 %copy-start = (bf16[8,2048]{1,0:T(8,128)(2,1)S(1)}, bf16[8,2048]{1,0:T(8,128)(2,1)}, u32[]{:S(2)}) copy-start(bf16[8,2048]{1,0:T(8,128)(2,1)} %get-tuple-element.34) | copy-start | bytes 98308

commit v2 on v1

--- a/solution.py
+++ b/solution.py
@@ -29,14 +29,14 @@
 
 
 def exchange_kernel(group_n, x_hbm, wq_hbm, wk_hbm, wv_hbm, wo_hbm, gains_ref, post_ref, cos_ref, sin_ref, cosd_ref, sind_ref, new_ref,
-                    qkv_ref, o_ref, rel_ref, relo_ref, knew_ref, vnew_ref, outd_ref,
-                    w_vm, x_vm, raw_vm, ssq_vm, stage_vm, qkv_vm, ostage_vm, wo_vm, qnew_vm, deco_vm, decp_vm,
-                    w_sem, x_sem, wo_sem, send_sem, recv_sem, rel_sem, fwd_sem, load_sem, osend_sem, orecv_sem, relo_sem, decs_sem, decr_sem):
+                    qkv_ref, o_ref, relkv_ref, relq_ref, relo_ref, kvp_ref, knew_ref, vnew_ref, outd_ref,
+                    w_vm, x_vm, raw_vm, ssq_vm, stage_vm, qkv_vm, ostage_vm, kvp_vm, olocal_vm, wo_vm, qnew_vm, deco_vm, decp_vm,
+                    w_sem, x_sem, wo_sem, send_sem, recvkv_sem, recvq_sem, relkv_sem, relq_sem, relo_sem, fwdkv_sem, fwdq_sem, fwdo_sem,
+                    load_sem, osend_sem, orecv_sem, kvps_sem, kvpr_sem, kvpl_sem, olocal_sem, decs_sem, decr_sem):
     n_batch, tok, width = x_hbm.shape
     cols = width // group_n
     heads = cols // HEAD_DIM
-    seq = tok * group_n
-    half = tok // 2
+    first_rows = CORES * tok
     chips = group_n // CORES
     me = lax.axis_index("sp")
     chip, core = me // CORES, me % CORES
@@ -45,8 +45,10 @@
     far = (chip + 2) % chips
     right_dev, left_dev = right * CORES + core, left * CORES + core
     partner = chip * CORES + (1 - core)
+    on_first = chip == 0
     w_hbm = (wq_hbm, wk_hbm, wv_hbm)
     scale2 = HEAD_DIM ** -0.5 * LOG2E
+    contract_last = (((1,), (1,)), ((), ()))
 
     def remote(src, dst, s_sem, r_sem, dev):
         return pltpu.make_async_remote_copy(src_ref=src, dst_ref=dst, send_sem=s_sem, recv_sem=r_sem,
@@ -55,6 +57,13 @@
     def drain(ref, sem):
         pltpu.make_async_copy(ref, ref, sem).wait()
 
+    def with_split(source, use):
+        mid, shift = tok // 2, tok // 8
+        for n, holds in ((mid - shift, source == 1), (mid + shift, source == chips - 1), (mid, source % 2 == 0)):
+            @pl.when(holds)
+            def _():
+                use(n)
+
     def w_copy(j):
         return pltpu.make_async_copy(w_hbm[j], w_vm.at[j], w_sem.at[j])
 
@@ -62,7 +71,7 @@
         return pltpu.make_async_copy(x_hbm.at[t], x_vm.at[lax.rem(t, 2)], x_sem.at[lax.rem(t, 2)])
 
     x_copy(0).start()
-    for j in range(3):
+    for j in (2, 1, 0):
         w_copy(j).start()
     wo_copy = pltpu.make_async_copy(wo_hbm.at[pl.ds(me * cols, cols)], wo_vm, wo_sem)
     wo_copy.start()
@@ -75,17 +84,35 @@
     def send_tensor(t, slot, j):
         rows = pl.ds(me * tok, tok)
         far_devs = pl.ds(far * CORES, CORES)
-        remote(stage_vm.at[slot, j, far_devs, pl.ds(0, half)], rel_ref.at[t, 0, :, j], send_sem.at[t], rel_sem.at[t], right_dev).start()
-        remote(stage_vm.at[slot, j, far_devs, pl.ds(half, half)], rel_ref.at[t, 1, :, j], send_sem.at[t], rel_sem.at[t], left_dev).start()
+        recv = recvkv_sem.at[t] if j else recvq_sem.at[t]
+
+        def two_hops(n):
+            for way, at, dev in ((0, pl.ds(0, n), right_dev), (1, pl.ds(n, tok - n), left_dev)):
+                dst, sem = (relkv_ref.at[t, way, :, j - 1, at], relkv_sem.at[t, way]) if j else (relq_ref.at[t, way, :, at], relq_sem.at[t, way])
+                remote(stage_vm.at[slot, j, far_devs, at], dst, send_sem.at[t], sem, dev).start()
+
+        with_split(chip, two_hops)
         for side in (right, left):
             for c in range(CORES):
                 dev = side * CORES + c
-                remote(stage_vm.at[slot, j, dev], qkv_ref.at[j, t, rows], send_sem.at[t], recv_sem.at[t], dev).start()
-        remote(stage_vm.at[slot, j, partner], qkv_ref.at[j, t, rows], send_sem.at[t], recv_sem.at[t], partner).start()
-        pltpu.make_async_copy(stage_vm.at[slot, j, me], qkv_ref.at[j, t, rows], recv_sem.at[t]).start()
+                remote(stage_vm.at[slot, j, dev], qkv_ref.at[j, t, rows], send_sem.at[t], recv, dev).start()
+        remote(stage_vm.at[slot, j, partner], qkv_ref.at[j, t, rows], send_sem.at[t], recv, partner).start()
+        pltpu.make_async_copy(stage_vm.at[slot, j, me], qkv_ref.at[j, t, rows], recv).start()
 
     def drain_sends(t):
-        drain(stage_vm.at[lax.rem(t, SLOTS), :, pl.ds(0, group_n - 1)], send_sem.at[t])
+        slot = lax.rem(t, SLOTS)
+
+        @pl.when(on_first)
+        def _():
+            drain(stage_vm.at[slot, pl.ds(1, 2), pl.ds(0, group_n - 1)], send_sem.at[t])
+
+        @pl.when(jnp.logical_not(on_first))
+        def _():
+            drain(stage_vm.at[slot, :, pl.ds(0, group_n - 1)], send_sem.at[t])
+
+        @pl.when(me == 0)
+        def _():
+            drain(stage_vm.at[slot, pl.ds(1, 2)], kvps_sem.at[t])
 
     def project(t):
         slot = lax.rem(t, SLOTS)
@@ -101,12 +128,13 @@
             x_copy(t + 1).start()
 
         x_slot = lax.rem(t, 2)
-        for j in range(3):
+        for j in (2, 1, 0):
             @pl.when(t == 0)
             def _():
                 w_copy(j).wait()
 
-            ssq_vm[...] = jnp.zeros_like(ssq_vm)
+            if j < 2:
+                ssq_vm[...] = jnp.zeros_like(ssq_vm)
 
             def col_tile(n, _):
                 at = pl.ds(pl.multiple_of(n * COL_TILE, COL_TILE), COL_TILE)
@@ -132,22 +160,66 @@
                     return 0
 
                 lax.fori_loop(0, group_n, group_tile, 0)
-            send_tensor(t, slot, j)
+            if j:
+                send_tensor(t, slot, j)
+            else:
+                @pl.when(jnp.logical_not(on_first))
+                def _():
+                    send_tensor(t, slot, j)
+
+        @pl.when(me == 0)
+        def _():
+            remote(stage_vm.at[slot, pl.ds(1, 2)], kvp_ref.at[t], kvps_sem.at[t], kvpr_sem.at[t], partner).start()
+
+    def relay_ways(use):
+        with_split(left, lambda n: use(0, left, left_dev, right, 0, n))
+        with_split(right, lambda n: use(1, right, right_dev, left, n, tok - n))
 
     def forward(b):
-        drain(rel_ref.at[b], rel_sem.at[b])
-        for way, came, to, first in ((0, left_dev, right, 0), (1, right_dev, left, half)):
+        def way_kv(way, source, source_dev, to, first, n):
+            at, dst_rows = pl.ds(first, n), pl.ds(source_dev * tok + first, n)
+            drain(relkv_ref.at[b, way, :, :, at], relkv_sem.at[b, way])
             for c in range(CORES):
-                remote(rel_ref.at[b, way, c], qkv_ref.at[:, b, pl.ds(came * tok + first, half)], fwd_sem.at[0], recv_sem.at[b], to * CORES + c).start()
+                remote(relkv_ref.at[b, way, c, :, at], qkv_ref.at[pl.ds(1, 2), b, dst_rows], fwdkv_sem.at[way], recvkv_sem.at[b], to * CORES + c).start()
+
+            @pl.when(source != 0)
+            def _():
+                drain(relq_ref.at[b, way, :, at], relq_sem.at[b, way])
+                for c in range(CORES):
+                    remote(relq_ref.at[b, way, c, at], qkv_ref.at[0, b, dst_rows], fwdq_sem.at[way], recvq_sem.at[b], to * CORES + c).start()
+
+        relay_ways(way_kv)
 
     def forward_o(b):
-        drain(relo_ref.at[b], relo_sem.at[b])
-        for way, came, to, first in ((0, left_dev, right, 0), (1, right_dev, left, half)):
-            for c in range(CORES):
-                remote(relo_ref.at[b, way, c], o_ref.at[b, came, pl.ds(first, half)], fwd_sem.at[1], orecv_sem.at[b], to * CORES + c).start()
+        def way_o(way, source, source_dev, to, first, n):
+            at = pl.ds(first, n)
+
+            @pl.when(to != 0)
+            def _():
+                drain(relo_ref.at[b, way, :, at], relo_sem.at[b, way])
+                for c in range(CORES):
+                    remote(relo_ref.at[b, way, c, at], o_ref.at[b, source_dev, at], fwdo_sem.at[way], orecv_sem.at[b], to * CORES + c).start()
+
+        relay_ways(way_o)
+
+    def drain_forwards():
+        def way_all(way, source, source_dev, to, first, n):
+            at = pl.ds(first, n)
+            drain(relkv_ref.at[:, way, :, :, at], fwdkv_sem.at[way])
+
+            @pl.when(source != 0)
+            def _():
+                drain(relq_ref.at[:, way, :, at], fwdq_sem.at[way])
+
+            @pl.when(to != 0)
+            def _():
+                drain(relo_ref.at[:, way, :, at], fwdo_sem.at[way])
+
+        relay_ways(way_all)
 
     def send_o(b, slot, dev):
         src = ostage_vm.at[slot, pl.ds(dev * tok, tok)]
+        c = dev % CORES
         away = lax.rem(dev // CORES - chip + chips, chips)
 
         @pl.when(dev == me)
@@ -160,9 +232,16 @@
 
         @pl.when(away == 2)
         def _():
-            c = dev % CORES
-            remote(ostage_vm.at[slot, pl.ds(dev * tok, half)], relo_ref.at[b, 0, c], osend_sem.at[b], relo_sem.at[b], right_dev).start()
-            remote(ostage_vm.at[slot, pl.ds(dev * tok + half, half)], relo_ref.at[b, 1, c], osend_sem.at[b], relo_sem.at[b], left_dev).start()
+            def two_hops(n):
+                remote(ostage_vm.at[slot, pl.ds(dev * tok, n)], relo_ref.at[b, 0, c, pl.ds(0, n)],
+                       osend_sem.at[b], relo_sem.at[b, 0], right_dev).start()
+                remote(ostage_vm.at[slot, pl.ds(dev * tok + n, tok - n)], relo_ref.at[b, 1, c, pl.ds(n, tok - n)],
+                       osend_sem.at[b], relo_sem.at[b, 1], left_dev).start()
+
+            with_split(chip, two_hops)
+
+    def drain_o_sends(b):
+        drain(ostage_vm.at[lax.rem(b, 2), pl.ds(first_rows, (group_n - CORES) * tok)], osend_sem.at[b])
 
     def new_row():
         def full(j):
@@ -185,41 +264,75 @@
         vnew_ref[...] = jnp.dot(new_ref[...], w_vm[2, :, own], preferred_element_type=jnp.float32).astype(jnp.bfloat16)
         deco_vm[...] = jnp.zeros_like(deco_vm)
 
+    def block_attention(q, k_diag, v_diag, k_past, v_past):
+        keep = lax.broadcasted_iota(jnp.int32, (tok, tok), 0) >= lax.broadcasted_iota(jnp.int32, (tok, tok), 1)
+        diag = lax.dot_general(q, k_diag, contract_last, preferred_element_type=jnp.float32)
+        diag = jnp.where(keep, diag, -jnp.inf)
+        top = jnp.max(diag, axis=1, keepdims=True)
+        if k_past is not None:
+            past = lax.dot_general(q, k_past, contract_last, preferred_element_type=jnp.float32)
+            top = jnp.maximum(top, jnp.max(past, axis=1, keepdims=True))
+            past = jnp.exp2((past - top) * scale2)
+        diag = jnp.exp2((diag - top) * scale2)
+        total = jnp.sum(diag, axis=1, keepdims=True)
+        if k_past is not None:
+            total = total + jnp.sum(past, axis=1, keepdims=True)
+        inv = 1.0 / total
+        out = jnp.dot((diag * inv).astype(jnp.bfloat16), v_diag, preferred_element_type=jnp.float32)
+        if k_past is not None:
+            out = out + jnp.dot((past * inv).astype(jnp.bfloat16), v_past, preferred_element_type=jnp.float32)
+        return out.astype(jnp.bfloat16)
+
+    def attend_first(b):
+        slot = lax.rem(b, SLOTS)
+
+        @pl.when(b >= 1)
+        def _():
+            drain(olocal_vm, olocal_sem)
+
+        for which in range(CORES):
+            @pl.when(core == which)
+            def _():
+                if which:
+                    drain(kvp_ref.at[b], kvpr_sem.at[b])
+                    load = pltpu.make_async_copy(kvp_ref.at[b], kvp_vm, kvpl_sem)
+                    load.start()
+                    load.wait()
+
+                def group(g, _):
+                    for h in range(heads):
+                        at = slice(h * HEAD_DIM, (h + 1) * HEAD_DIM)
+                        past = (kvp_vm[0, g, :, at], kvp_vm[1, g, :, at]) if which else (None, None)
+                        olocal_vm[g, :, at] = block_attention(stage_vm[slot, 0, g, :, at], stage_vm[slot, 1, g, :, at], stage_vm[slot, 2, g, :, at], *past)
+                    return 0
+
+                lax.fori_loop(0, group_n, group, 0)
+
+        pltpu.make_async_copy(olocal_vm, o_ref.at[b], olocal_sem).start()
+
     def attend(b):
         slot = lax.rem(b, 2)
-        drain(qkv_ref.at[:, b], recv_sem.at[b])
-        load = pltpu.make_async_copy(qkv_ref.at[:, b], qkv_vm, load_sem)
-        load.start()
+        q_rows = pl.ds(first_rows, (group_n - CORES) * tok)
+        drain(qkv_ref.at[pl.ds(1, 2), b], recvkv_sem.at[b])
+        drain(qkv_ref.at[0, b, q_rows], recvq_sem.at[b])
+        load_kv = pltpu.make_async_copy(qkv_ref.at[pl.ds(1, 2), b], qkv_vm.at[pl.ds(1, 2)], load_sem.at[0])
+        load_q = pltpu.make_async_copy(qkv_ref.at[0, b, q_rows], qkv_vm.at[0, q_rows], load_sem.at[1])
+        load_kv.start()
+        load_q.start()
 
         @pl.when(b >= 2)
         def _():
-            drain(ostage_vm.at[slot], osend_sem.at[b - 2])
-
-        load.wait()
-        keep = lax.broadcasted_iota(jnp.int32, (tok, tok), 0) >= lax.broadcasted_iota(jnp.int32, (tok, tok), 1)
-        contract_last = (((1,), (1,)), ((), ()))
-        for blk in range(group_n):
+            drain_o_sends(b - 2)
+
+        load_kv.wait()
+        load_q.wait()
+        for blk in range(CORES, group_n):
             rows = slice(blk * tok, (blk + 1) * tok)
 
             def one_head(h, _):
                 at = pl.ds(pl.multiple_of(h * HEAD_DIM, HEAD_DIM), HEAD_DIM)
-                q = qkv_vm[0, rows, at]
-                diag = lax.dot_general(q, qkv_vm[1, rows, at], contract_last, preferred_element_type=jnp.float32)
-                diag = jnp.where(keep, diag, -jnp.inf)
-                top = jnp.max(diag, axis=1, keepdims=True)
-                if blk:
-                    past = lax.dot_general(q, qkv_vm[1, :blk * tok, at], contract_last, preferred_element_type=jnp.float32)
-                    top = jnp.maximum(top, jnp.max(past, axis=1, keepdims=True))
-                    past = jnp.exp2((past - top) * scale2)
-                diag = jnp.exp2((diag - top) * scale2)
-                total = jnp.sum(diag, axis=1, keepdims=True)
-                if blk:
-                    total = total + jnp.sum(past, axis=1, keepdims=True)
-                inv = 1.0 / total
-                out = jnp.dot((diag * inv).astype(jnp.bfloat16), qkv_vm[2, rows, at], preferred_element_type=jnp.float32)
-                if blk:
-                    out = out + jnp.dot((past * inv).astype(jnp.bfloat16), qkv_vm[2, :blk * tok, at], preferred_element_type=jnp.float32)
-                ostage_vm[slot, rows, at] = out.astype(jnp.bfloat16)
+                ostage_vm[slot, rows, at] = block_attention(qkv_vm[0, rows, at], qkv_vm[1, rows, at], qkv_vm[2, rows, at],
+                                                            qkv_vm[1, :blk * tok, at], qkv_vm[2, :blk * tok, at])
                 return 0
 
             lax.fori_loop(0, heads, one_head, 0)
@@ -262,6 +375,10 @@
         def _():
             forward_o(t - 3)
 
+        @pl.when(jnp.logical_and(on_first, jnp.logical_and(t >= 1, t <= n_batch)))
+        def _():
+            attend_first(t - 1)
+
         @pl.when(jnp.logical_and(t >= 2, t <= n_batch + 1))
         def _():
             attend(t - 2)
@@ -283,30 +400,39 @@
     for t in range(n_batch - SLOTS, n_batch):
         drain_sends(t)
     for b in range(n_batch - 2, n_batch):
-        drain(ostage_vm.at[b % 2], osend_sem.at[b])
-    drain(rel_ref, fwd_sem.at[0])
-    drain(relo_ref, fwd_sem.at[1])
-    for b in range(n_batch):
-        drain(o_ref.at[b, pl.ds(0, group_n - 1)], orecv_sem.at[b])
+        drain_o_sends(b)
+    drain_forwards()
+
+    @pl.when(on_first)
+    def _():
+        drain(olocal_vm, olocal_sem)
+
+    @pl.when(jnp.logical_not(on_first))
+    def _():
+        for b in range(n_batch):
+            drain(o_ref.at[b, pl.ds(0, group_n - 1)], orecv_sem.at[b])
 
 
 def output_kernel(o_ref, x_ref, wo_ref, post_ref, k_ref, v_ref, knew_ref, vnew_ref, out_ref, kc_ref, vc_ref, raw_vm):
-    group_n, tok, cols = o_ref.shape[1:]
+    n_seq, group_n, tok, cols = o_ref.shape
     width = group_n * cols
     heads = cols // HEAD_DIM
-    o_all = jnp.concatenate([o_ref[0, g] for g in range(group_n)], axis=1)
-    ssq = jnp.zeros((tok, 1), jnp.float32)
+    o_all = jnp.concatenate([o_ref[:, g].reshape(n_seq * tok, cols) for g in range(group_n)], axis=1)
+    ssq = jnp.zeros((n_seq * tok, 1), jnp.float32)
     for n in range(width // COL_TILE):
         at = slice(n * COL_TILE, (n + 1) * COL_TILE)
         acc = jnp.dot(o_all, wo_ref[:, at], preferred_element_type=jnp.float32)
         raw_vm[:, at] = acc
         ssq = ssq + jnp.sum(acc * acc, axis=1, keepdims=True)
     inv = lax.rsqrt(ssq / width + NORM_EPS)
-    out_ref[0] = (x_ref[0].astype(jnp.float32) + raw_vm[...] * inv * post_ref[...]).astype(jnp.bfloat16)
+    for i in range(n_seq):
+        at = slice(i * tok, (i + 1) * tok)
+        out_ref[i] = (x_ref[i].astype(jnp.float32) + raw_vm[at] * inv[at] * post_ref[...]).astype(jnp.bfloat16)
     seq = k_ref.shape[2]
     for src, new, to in ((k_ref, knew_ref, kc_ref), (v_ref, vnew_ref, vc_ref)):
-        to[0, :seq] = src[0, 0].reshape(seq, heads, HEAD_DIM)
-        to[0, seq:] = new[0].reshape(1, heads, HEAD_DIM)
+        for i in range(n_seq):
+            to[i, :seq] = src[0, i].reshape(seq, heads, HEAD_DIM)
+            to[i, seq:] = new[i].reshape(1, heads, HEAD_DIM)
 
 
 def solution(mesh):
@@ -317,7 +443,6 @@
         cols = width // group_n
         heads = cols // HEAD_DIM
         seq = tok * group_n
-        half = tok // 2
         bf16, f32 = jnp.bfloat16, jnp.float32
         cos_p, sin_p = rope_tables(lax.axis_index("sp") * tok + jnp.arange(tok))
         cos_d, sin_d = rope_tables(jnp.full((1,), seq))
@@ -326,19 +451,21 @@
         any_spec = pl.BlockSpec(memory_space=pl.ANY)
         vm_spec = pl.BlockSpec(memory_space=pltpu.VMEM)
         dma = pltpu.SemaphoreType.DMA
-        qkv, o_all, _, _, k_new, v_new, out_d = pl.pallas_call(
+        qkv, o_all, _, _, _, _, k_new, v_new, out_d = pl.pallas_call(
             functools.partial(exchange_kernel, group_n),
             out_shape=(
                 jax.ShapeDtypeStruct((3, n_batch, seq, cols), bf16),
                 jax.ShapeDtypeStruct((n_batch, group_n, tok, cols), bf16),
-                jax.ShapeDtypeStruct((n_batch, 2, CORES, 3, half, cols), bf16),
-                jax.ShapeDtypeStruct((n_batch, 2, CORES, half, cols), bf16),
+                jax.ShapeDtypeStruct((n_batch, 2, CORES, 2, tok, cols), bf16),
+                jax.ShapeDtypeStruct((n_batch, 2, CORES, tok, cols), bf16),
+                jax.ShapeDtypeStruct((n_batch, 2, CORES, tok, cols), bf16),
+                jax.ShapeDtypeStruct((n_batch, 2, group_n, tok, cols), bf16),
                 jax.ShapeDtypeStruct((n_batch, cols), bf16),
                 jax.ShapeDtypeStruct((n_batch, cols), bf16),
                 jax.ShapeDtypeStruct((n_batch, width), bf16),
             ),
             in_specs=[any_spec] * 5 + [vm_spec] * 7,
-            out_specs=(any_spec,) * 4 + (vm_spec,) * 3,
+            out_specs=(any_spec,) * 6 + (vm_spec,) * 3,
             scratch_shapes=[
                 pltpu.VMEM((3, width, width), bf16),
                 pltpu.VMEM((2, tok, width), bf16),
@@ -347,21 +474,24 @@
                 pltpu.VMEM((SLOTS, 3, group_n, tok, cols), bf16),
                 pltpu.VMEM((3, seq, cols), bf16),
                 pltpu.VMEM((2, seq, cols), bf16),
+                pltpu.VMEM((2, group_n, tok, cols), bf16),
+                pltpu.VMEM((group_n, tok, cols), bf16),
                 pltpu.VMEM((cols, width), bf16),
                 pltpu.VMEM((n_batch, cols), bf16),
                 pltpu.VMEM((n_batch, cols), f32),
                 pltpu.VMEM((group_n, n_batch, width), bf16),
                 dma((3,)), dma((2,)), dma,
-                dma((n_batch,)), dma((n_batch,)), dma((n_batch,)), dma((2,)), dma,
-                dma((n_batch,)), dma((n_batch,)), dma((n_batch,)), dma, dma,
+                dma((n_batch,)), dma((n_batch,)), dma((n_batch,)), dma((n_batch, 2)), dma((n_batch, 2)), dma((n_batch, 2)), dma((2,)), dma((2,)), dma((2,)),
+                dma((2,)), dma((n_batch,)), dma((n_batch,)), dma((n_batch,)), dma((n_batch,)), dma, dma, dma, dma,
             ],
             compiler_params=pltpu.CompilerParams(collective_id=0, has_side_effects=True, vmem_limit_bytes=VMEM_BYTES),
         )(prompt_blk, w_q, w_k, w_v, w_o, gains, post, cos_p, sin_p, cos_d, sin_d, new_rows)
 
-        row = lambda shape, at: pl.BlockSpec((1,) + shape, lambda b: (b,) + at)
+        pair = 2 if n_batch % 2 == 0 else 1
+        row = lambda shape, at: pl.BlockSpec((pair,) + shape, lambda b: (b,) + at)
         out_p, k_cache, v_cache = pl.pallas_call(
             output_kernel,
-            grid=(n_batch,),
+            grid=(n_batch // pair,),
             out_shape=(
                 jax.ShapeDtypeStruct((n_batch, tok, width), bf16),
                 jax.ShapeDtypeStruct((n_batch, seq + 1, heads, HEAD_DIM), bf16),
@@ -372,13 +502,13 @@
                 row((tok, width), (0, 0)),
                 vm_spec,
                 vm_spec,
-                pl.BlockSpec((1, 1, seq, cols), lambda b: (1, b, 0, 0)),
-                pl.BlockSpec((1, 1, seq, cols), lambda b: (2, b, 0, 0)),
+                pl.BlockSpec((1, pair, seq, cols), lambda b: (1, b, 0, 0)),
+                pl.BlockSpec((1, pair, seq, cols), lambda b: (2, b, 0, 0)),
                 row((1, cols), (0, 0)),
                 row((1, cols), (0, 0)),
             ],
             out_specs=(row((tok, width), (0, 0)), row((seq + 1, heads, HEAD_DIM), (0, 0, 0)), row((seq + 1, heads, HEAD_DIM), (0, 0, 0))),
-            scratch_shapes=[pltpu.VMEM((tok, width), f32)],
+            scratch_shapes=[pltpu.VMEM((pair * tok, width), f32)],
             compiler_params=pltpu.CompilerParams(vmem_limit_bytes=VMEM_BYTES),
         )(o_all, prompt_blk, w_o, post, qkv, qkv, k_new[:, None], v_new[:, None])
         return out_p, k_cache, v_cache, out_d

time: 428 us -> 404 us (0.944)
  Pallas kernels: 419 us -> 396 us
    pallas_call x1, Pallas kernels: 387 us -> 363 us  [device_step(): pl.pallas_call(functools.partial(exchange_kernel, group_n), out_shape=(ja...]
where the time goes in v2:
time: 404 us
  Pallas kernels  396 us (98%)
    pallas_call x1, Pallas kernels, device_step(): pl.pallas_call(functools.partial(exchange_kernel, group_n), out_shape=(ja...  363 us
    pallas_call x1, Pallas kernels, device_step(): pl.pallas_call(output_kernel, grid=(n_batch // pair,), out_shape=(jax.Sha...  32.9 us

profile of v2, /device:TPU:81, one launch (start us, length us, event | category | flops | bytes accessed | tf_op | source)
XLA Modules:
  0.0 403.5 jit_solution(16879619933280790921)
XLA Ops:
  0.7 0.6 pad_maximum_fusion.3.cosd_ref
  1.3 0.1 fusion.1
  1.4 0.6 pad_maximum_fusion.4.sind_ref
  2.0 1.3 pad_maximum_fusion.2.gains_ref
  3.3 0.5 fusion
  3.9 0.8 pad_maximum_fusion
  4.7 362.7 %shard_map.120 = (bf16[3,8,2048,256]{3,2,1,0:T(8,128)(2,1)}, bf16[8,8,256,256]{3,2,1,0:T(8,128)(2,1)}, bf16[8,2,2,2,256,256]{5,4,3,2,1,0:T(8,128)(2,1)}, bf16[8,...) custom-call(bf16[8,256,2048]{2,1,0:T(8,128)(2,1)} %x_ref.1, ...), custom_call_target="tpu_custom_call" | custom-call | tf_op jit(solution)/shard_map/pallas_call | solution.py:454
  367.4 1.3 copy.13.knew_ref
  368.7 1.3 copy.14.vnew_ref
  369.9 0.0 copy-start
  369.9 32.9 %shard_map.121 = (bf16[8,256,2048]{2,1,0:T(8,128)(2,1)}, bf16[8,2049,2,128]{3,2,1,0:T(2,128)(2,1)}, bf16[8,2049,2,128]{3,2,1,0:T(2,128)(2,1)}) custom-call(bf16[8,8,256,256]{3,2,1,0:T(8,128)(2,1)} %get-tuple-element.12.o_ref, bf16[8,256,2048]{2,1,0:T(8,128)(2,1)} %x_ref.1, bf16[2048,2048]{1,0:T(8,128)(2,1)} %wo_ref.1, f32[1,2048]{1,0:T(1,128)} %bitcast.6, ...), custom_call_target="tpu_custom_call" | custom-call | tf_op jit(solution)/shard_map/pallas_call | solution.py:492
  402.9 0.0 copy-done
  402.9 0.6 copy.16
  (3 shorter events, 0.1 us)
Async XLA Ops:
  369.9 32.9 %copy-start = (bf16[8,2048]{1,0:T(8,128)(2,1)S(1)}, bf16[8,2048]{1,0:T(8,128)(2,1)}, u32[]{:S(2)}) copy-start(bf16[8,2048]{1,0:T(8,128)(2,1)} %get-tuple-element.34) | copy-start | bytes 98308

commit v3 on v2

--- a/solution.py
+++ b/solution.py
@@ -13,26 +13,28 @@
 CORES = 2
 LOG2E = 1.4426950408889634
 SLOTS = 3
+LATE = 2
 COL_TILE = 512
 VMEM_BYTES = 66_000_000
 
 
 def rope_tables(positions):
-    inv_freq = ROPE_THETA ** (-jnp.arange(0, HEAD_DIM, 2).astype(jnp.float32) / HEAD_DIM)
+    lane = jnp.arange(HEAD_DIM) % (HEAD_DIM // 2)
+    inv_freq = ROPE_THETA ** (-(2 * lane).astype(jnp.float32) / HEAD_DIM)
     angles = positions.astype(jnp.float32)[:, None] * inv_freq[None, :]
-    cos_t, sin_t = jnp.cos(angles), jnp.sin(angles)
-    return jnp.concatenate([cos_t, cos_t], axis=-1), jnp.concatenate([-sin_t, sin_t], axis=-1)
+    sign = jnp.where(jnp.arange(HEAD_DIM) < HEAD_DIM // 2, -1.0, 1.0)
+    return jnp.cos(angles), jnp.sin(angles) * sign[None, :]
 
 
 def rotate(values, cos_t, sin_t):
     return values * cos_t + pltpu.roll(values, HEAD_DIM // 2, 1) * sin_t
 
 
-def exchange_kernel(group_n, x_hbm, wq_hbm, wk_hbm, wv_hbm, wo_hbm, gains_ref, post_ref, cos_ref, sin_ref, cosd_ref, sind_ref, new_ref,
-                    qkv_ref, o_ref, relkv_ref, relq_ref, relo_ref, kvp_ref, knew_ref, vnew_ref, outd_ref,
-                    w_vm, x_vm, raw_vm, ssq_vm, stage_vm, qkv_vm, ostage_vm, kvp_vm, olocal_vm, wo_vm, qnew_vm, deco_vm, decp_vm,
+def exchange_kernel(group_n, x_hbm, wq_hbm, wk_hbm, wv_hbm, wo_hbm, qgain_ref, kgain_ref, post_ref, cos_ref, sin_ref, new_ref,
+                    qkv_ref, o_ref, relkv_ref, relq_ref, relo_ref, kvp_ref, outp_ref, knew_ref, vnew_ref, outd_ref,
+                    w_vm, x_vm, raw_vm, ssq_vm, stage_vm, qkv_vm, ostage_vm, kvp_vm, olocal_vm, wo_vm, oin_vm, xo_vm, outv_vm, qnew_vm, knew_vm, vnew_vm, deco_vm, decp_vm,
                     w_sem, x_sem, wo_sem, send_sem, recvkv_sem, recvq_sem, relkv_sem, relq_sem, relo_sem, fwdkv_sem, fwdq_sem, fwdo_sem,
-                    load_sem, osend_sem, orecv_sem, kvps_sem, kvpr_sem, kvpl_sem, olocal_sem, decs_sem, decr_sem):
+                    load_sem, osend_sem, orecv_sem, kvps_sem, kvpr_sem, kvpl_sem, olocal_sem, oin_sem, xo_sem, outv_sem, decs_sem, decr_sem):
     n_batch, tok, width = x_hbm.shape
     cols = width // group_n
     heads = cols // HEAD_DIM
@@ -47,6 +49,7 @@
     partner = chip * CORES + (1 - core)
     on_first = chip == 0
     w_hbm = (wq_hbm, wk_hbm, wv_hbm)
+    gains = (qgain_ref, kgain_ref)
     scale2 = HEAD_DIM ** -0.5 * LOG2E
     contract_last = (((1,), (1,)), ((), ()))
 
@@ -73,7 +76,7 @@
     x_copy(0).start()
     for j in (2, 1, 0):
         w_copy(j).start()
-    wo_copy = pltpu.make_async_copy(wo_hbm.at[pl.ds(me * cols, cols)], wo_vm, wo_sem)
+    wo_copy = pltpu.make_async_copy(wo_hbm, wo_vm, wo_sem)
     wo_copy.start()
 
     barrier = pltpu.get_barrier_semaphore()
@@ -155,8 +158,8 @@
                 def group_tile(n, _):
                     for h in range(heads):
                         at = pl.ds(pl.multiple_of(n * cols + h * HEAD_DIM, HEAD_DIM), HEAD_DIM)
-                        normed = raw_vm[:, at] * inv * gains_ref[j:j + 1, at]
-                        stage_vm[slot, j, n, :, h * HEAD_DIM:(h + 1) * HEAD_DIM] = rotate(normed, cos_ref[...], sin_ref[...]).astype(jnp.bfloat16)
+                        normed = raw_vm[:, at] * inv * gains[j][:, at]
+                        stage_vm[slot, j, n, :, h * HEAD_DIM:(h + 1) * HEAD_DIM] = rotate(normed, cos_ref[:tok], sin_ref[:tok]).astype(jnp.bfloat16)
                     return 0
 
                 lax.fori_loop(0, group_n, group_tile, 0)
@@ -254,14 +257,17 @@
             return lax.rsqrt(ssq / width + NORM_EPS)
 
         own = pl.ds(pl.multiple_of(me * cols, cols), cols)
-        for j, to in ((0, qnew_vm), (1, knew_ref)):
+        for j, to in ((0, qnew_vm), (1, knew_vm)):
             inv = full(j)
             raw = jnp.dot(new_ref[...], w_vm[j, :, own], preferred_element_type=jnp.float32)
-            normed = raw * inv * gains_ref[j:j + 1, own]
+            normed = raw * inv * gains[j][:, own]
             for h in range(heads):
                 at = slice(h * HEAD_DIM, (h + 1) * HEAD_DIM)
-                to[:, at] = rotate(normed[:, at], cosd_ref[...], sind_ref[...]).astype(jnp.bfloat16)
-        vnew_ref[...] = jnp.dot(new_ref[...], w_vm[2, :, own], preferred_element_type=jnp.float32).astype(jnp.bfloat16)
+                to[:, at] = rotate(normed[:, at], cos_ref[tok:tok + 1], sin_ref[tok:tok + 1]).astype(jnp.bfloat16)
+        vnew_vm[...] = jnp.dot(new_ref[...], w_vm[2, :, own], preferred_element_type=jnp.float32).astype(jnp.bfloat16)
+        for b in range(n_batch):
+            knew_ref[b] = knew_vm[b:b + 1]
+            vnew_ref[b] = vnew_vm[b:b + 1]
         deco_vm[...] = jnp.zeros_like(deco_vm)
 
     def block_attention(q, k_diag, v_diag, k_past, v_past):
@@ -343,17 +349,58 @@
             at = slice(h * HEAD_DIM, (h + 1) * HEAD_DIM)
             q = qnew_vm[:, at]
             past = lax.dot_general(q, qkv_vm[1, :, at], contract_last, preferred_element_type=jnp.float32)
-            last = jnp.sum(q.astype(jnp.float32) * knew_ref[:, at].astype(jnp.float32), axis=1, keepdims=True)
+            last = jnp.sum(q.astype(jnp.float32) * knew_vm[:, at].astype(jnp.float32), axis=1, keepdims=True)
             top = jnp.maximum(jnp.max(past, axis=1, keepdims=True), last)
             past, last = jnp.exp2((past - top) * scale2), jnp.exp2((last - top) * scale2)
             inv = 1.0 / (jnp.sum(past, axis=1, keepdims=True) + last)
             out = jnp.dot((past * inv).astype(jnp.bfloat16), qkv_vm[2, :, at], preferred_element_type=jnp.float32)
-            out = out + (last * inv).astype(jnp.bfloat16).astype(jnp.float32) * vnew_ref[:, at].astype(jnp.float32)
+            out = out + (last * inv).astype(jnp.bfloat16).astype(jnp.float32) * vnew_vm[:, at].astype(jnp.float32)
             deco_vm[:, at] = jnp.where(mine, out, deco_vm[:, at])
 
+    def output_rows(b):
+        @pl.when(jnp.logical_not(on_first))
+        def _():
+            drain(o_ref.at[b, pl.ds(0, group_n - 1)], orecv_sem.at[b])
+
+        for g in range(group_n):
+            pltpu.make_async_copy(o_ref.at[b, g], oin_vm.at[:, pl.ds(g * cols, cols)], oin_sem).start()
+        load_x = pltpu.make_async_copy(x_hbm.at[b], xo_vm, xo_sem)
+        load_x.start()
+
+        @pl.when(b >= 1)
+        def _():
+            drain(outv_vm, outv_sem)
+
+        @pl.when(b == 0)
+        def _():
+            wo_copy.wait()
+
+        ssq_vm[...] = jnp.zeros_like(ssq_vm)
+        drain(oin_vm, oin_sem)
+
+        def col_tile(n, _):
+            at = pl.ds(pl.multiple_of(n * COL_TILE, COL_TILE), COL_TILE)
+            acc = jnp.dot(oin_vm[...], wo_vm[:, at], preferred_element_type=jnp.float32)
+            raw_vm[:, at] = acc
+            sq = acc * acc
+            ssq_vm[...] += sum(sq[:, i * HEAD_DIM:(i + 1) * HEAD_DIM] for i in range(COL_TILE // HEAD_DIM))
+            return 0
+
+        lax.fori_loop(0, width // COL_TILE, col_tile, 0)
+        inv = lax.rsqrt(jnp.sum(ssq_vm[...], axis=1, keepdims=True) / width + NORM_EPS)
+        load_x.wait()
+
+        def out_tile(n, _):
+            at = pl.ds(pl.multiple_of(n * cols, cols), cols)
+            outv_vm[:, at] = (xo_vm[:, at].astype(jnp.float32) + raw_vm[:, at] * inv * post_ref[:, at]).astype(jnp.bfloat16)
+            return 0
+
+        lax.fori_loop(0, group_n, out_tile, 0)
+        pltpu.make_async_copy(outv_vm, outp_ref.at[b], outv_sem).start()
+
     def send_part():
-        wo_copy.wait()
-        part = jnp.dot(deco_vm[...].astype(jnp.bfloat16), wo_vm[...], preferred_element_type=jnp.float32)
+        own = pl.ds(pl.multiple_of(me * cols, cols), cols)
+        part = jnp.dot(deco_vm[...].astype(jnp.bfloat16), wo_vm[own], preferred_element_type=jnp.float32)
         decp_vm[me] = part.astype(jnp.bfloat16)
         for step in range(1, group_n):
             remote(decp_vm.at[me], decp_vm.at[me], decs_sem, decr_sem, lax.rem(me + step, group_n)).start()
@@ -367,25 +414,29 @@
         def _():
             new_row()
 
-        @pl.when(jnp.logical_and(t >= 1, t <= n_batch))
-        def _():
-            forward(t - 1)
-
-        @pl.when(t >= 3)
-        def _():
-            forward_o(t - 3)
-
-        @pl.when(jnp.logical_and(on_first, jnp.logical_and(t >= 1, t <= n_batch)))
+        @pl.when(t >= 2)
+        def _():
+            forward_o(t - 2)
+
+        @pl.when(jnp.logical_and(on_first, t >= 1))
         def _():
             attend_first(t - 1)
 
-        @pl.when(jnp.logical_and(t >= 2, t <= n_batch + 1))
-        def _():
-            attend(t - 2)
+        @pl.when(t >= 1)
+        def _():
+            attend(t - 1)
+
+        @pl.when(t < n_batch)
+        def _():
+            forward(t)
+
+        @pl.when(jnp.logical_and(t >= 3, t < n_batch + 3 - LATE))
+        def _():
+            output_rows(t - 3)
 
         return 0
 
-    lax.fori_loop(0, n_batch + 2, step, 0)
+    lax.fori_loop(0, n_batch + 1, step, 0)
     send_part()
     forward_o(n_batch - 1)
 
@@ -409,30 +460,47 @@
 
     @pl.when(jnp.logical_not(on_first))
     def _():
-        for b in range(n_batch):
+        for b in range(n_batch - LATE, n_batch):
             drain(o_ref.at[b, pl.ds(0, group_n - 1)], orecv_sem.at[b])
 
-
-def output_kernel(o_ref, x_ref, wo_ref, post_ref, k_ref, v_ref, knew_ref, vnew_ref, out_ref, kc_ref, vc_ref, raw_vm):
-    n_seq, group_n, tok, cols = o_ref.shape
+    drain(outv_vm, outv_sem)
+
+
+def output_kernel(o_ref, x_ref, wo_hbm, post_ref, outp_ref, k_ref, v_ref, knew_ref, vnew_ref, out_ref, kc_ref, vc_ref, wo_vm, raw_vm, wo_sem):
+    _, group_n, tok, cols = o_ref.shape
     width = group_n * cols
     heads = cols // HEAD_DIM
-    o_all = jnp.concatenate([o_ref[:, g].reshape(n_seq * tok, cols) for g in range(group_n)], axis=1)
-    ssq = jnp.zeros((n_seq * tok, 1), jnp.float32)
-    for n in range(width // COL_TILE):
-        at = slice(n * COL_TILE, (n + 1) * COL_TILE)
-        acc = jnp.dot(o_all, wo_ref[:, at], preferred_element_type=jnp.float32)
-        raw_vm[:, at] = acc
-        ssq = ssq + jnp.sum(acc * acc, axis=1, keepdims=True)
-    inv = lax.rsqrt(ssq / width + NORM_EPS)
-    for i in range(n_seq):
-        at = slice(i * tok, (i + 1) * tok)
-        out_ref[i] = (x_ref[i].astype(jnp.float32) + raw_vm[at] * inv[at] * post_ref[...]).astype(jnp.bfloat16)
+    b, n_batch = pl.program_id(0), pl.num_programs(0)
+    wo_copy = pltpu.make_async_copy(wo_hbm, wo_vm, wo_sem)
+
+    @pl.when(b == 0)
+    def _():
+        wo_copy.start()
+
+    @pl.when(b < n_batch - LATE)
+    def _():
+        out_ref[...] = outp_ref[...]
+
+    @pl.when(b == n_batch - LATE)
+    def _():
+        wo_copy.wait()
+
+    @pl.when(b >= n_batch - LATE)
+    def _():
+        o_all = jnp.concatenate([o_ref[0, g] for g in range(group_n)], axis=1)
+        ssq = jnp.zeros((tok, 1), jnp.float32)
+        for n in range(width // COL_TILE):
+            at = slice(n * COL_TILE, (n + 1) * COL_TILE)
+            acc = jnp.dot(o_all, wo_vm[:, at], preferred_element_type=jnp.float32)
+            raw_vm[:, at] = acc
+            ssq = ssq + jnp.sum(acc * acc, axis=1, keepdims=True)
+        inv = lax.rsqrt(ssq / width + NORM_EPS)
+        out_ref[0] = (x_ref[0].astype(jnp.float32) + raw_vm[...] * inv * post_ref[...]).astype(jnp.bfloat16)
+
     seq = k_ref.shape[2]
     for src, new, to in ((k_ref, knew_ref, kc_ref), (v_ref, vnew_ref, vc_ref)):
-        for i in range(n_seq):
-            to[i, :seq] = src[0, i].reshape(seq, heads, HEAD_DIM)
-            to[i, seq:] = new[i].reshape(1, heads, HEAD_DIM)
+        to[0, :seq] = src[0, 0].reshape(seq, heads, HEAD_DIM)
+        to[0, seq:] = new[0].reshape(1, heads, HEAD_DIM)
 
 
 def solution(mesh):
@@ -444,14 +512,13 @@
         heads = cols // HEAD_DIM
         seq = tok * group_n
         bf16, f32 = jnp.bfloat16, jnp.float32
-        cos_p, sin_p = rope_tables(lax.axis_index("sp") * tok + jnp.arange(tok))
-        cos_d, sin_d = rope_tables(jnp.full((1,), seq))
-        gains = jnp.stack([q_norm_w, k_norm_w])
-        post = post_norm_w[None]
+        step = jnp.arange(tok + 8)
+        cos_t, sin_t = rope_tables(jnp.where(step < tok, lax.axis_index("sp") * tok + step, seq))
+        q_gain, k_gain, post = q_norm_w[None], k_norm_w[None], post_norm_w[None]
         any_spec = pl.BlockSpec(memory_space=pl.ANY)
         vm_spec = pl.BlockSpec(memory_space=pltpu.VMEM)
         dma = pltpu.SemaphoreType.DMA
-        qkv, o_all, _, _, _, _, k_new, v_new, out_d = pl.pallas_call(
+        qkv, o_all, _, _, _, _, out_early, k_new, v_new, out_d = pl.pallas_call(
             functools.partial(exchange_kernel, group_n),
             out_shape=(
                 jax.ShapeDtypeStruct((3, n_batch, seq, cols), bf16),
@@ -460,12 +527,13 @@
                 jax.ShapeDtypeStruct((n_batch, 2, CORES, tok, cols), bf16),
                 jax.ShapeDtypeStruct((n_batch, 2, CORES, tok, cols), bf16),
                 jax.ShapeDtypeStruct((n_batch, 2, group_n, tok, cols), bf16),
-                jax.ShapeDtypeStruct((n_batch, cols), bf16),
-                jax.ShapeDtypeStruct((n_batch, cols), bf16),
+                jax.ShapeDtypeStruct((n_batch - LATE, tok, width), bf16),
+                jax.ShapeDtypeStruct((n_batch, 1, cols), bf16),
+                jax.ShapeDtypeStruct((n_batch, 1, cols), bf16),
                 jax.ShapeDtypeStruct((n_batch, width), bf16),
             ),
-            in_specs=[any_spec] * 5 + [vm_spec] * 7,
-            out_specs=(any_spec,) * 6 + (vm_spec,) * 3,
+            in_specs=[any_spec] * 5 + [vm_spec] * 6,
+            out_specs=(any_spec,) * 7 + (vm_spec,) * 3,
             scratch_shapes=[
                 pltpu.VMEM((3, width, width), bf16),
                 pltpu.VMEM((2, tok, width), bf16),
@@ -476,41 +544,47 @@
                 pltpu.VMEM((2, seq, cols), bf16),
                 pltpu.VMEM((2, group_n, tok, cols), bf16),
                 pltpu.VMEM((group_n, tok, cols), bf16),
-                pltpu.VMEM((cols, width), bf16),
+                pltpu.VMEM((width, width), bf16),
+                pltpu.VMEM((tok, width), bf16),
+                pltpu.VMEM((tok, width), bf16),
+                pltpu.VMEM((tok, width), bf16),
+                pltpu.VMEM((n_batch, cols), bf16),
+                pltpu.VMEM((n_batch, cols), bf16),
                 pltpu.VMEM((n_batch, cols), bf16),
                 pltpu.VMEM((n_batch, cols), f32),
                 pltpu.VMEM((group_n, n_batch, width), bf16),
                 dma((3,)), dma((2,)), dma,
                 dma((n_batch,)), dma((n_batch,)), dma((n_batch,)), dma((n_batch, 2)), dma((n_batch, 2)), dma((n_batch, 2)), dma((2,)), dma((2,)), dma((2,)),
-                dma((2,)), dma((n_batch,)), dma((n_batch,)), dma((n_batch,)), dma((n_batch,)), dma, dma, dma, dma,
+                dma((2,)), dma((n_batch,)), dma((n_batch,)), dma((n_batch,)), dma((n_batch,)), dma, dma, dma, dma, dma, dma, dma,
             ],
             compiler_params=pltpu.CompilerParams(collective_id=0, has_side_effects=True, vmem_limit_bytes=VMEM_BYTES),
-        )(prompt_blk, w_q, w_k, w_v, w_o, gains, post, cos_p, sin_p, cos_d, sin_d, new_rows)
-
-        pair = 2 if n_batch % 2 == 0 else 1
-        row = lambda shape, at: pl.BlockSpec((pair,) + shape, lambda b: (b,) + at)
+        )(prompt_blk, w_q, w_k, w_v, w_o, q_gain, k_gain, post, cos_t, sin_t, new_rows)
+
+        row = lambda shape, at: pl.BlockSpec((1,) + shape, lambda b: (b,) + at)
+        late = n_batch - LATE
         out_p, k_cache, v_cache = pl.pallas_call(
             output_kernel,
-            grid=(n_batch // pair,),
+            grid=(n_batch,),
             out_shape=(
                 jax.ShapeDtypeStruct((n_batch, tok, width), bf16),
                 jax.ShapeDtypeStruct((n_batch, seq + 1, heads, HEAD_DIM), bf16),
                 jax.ShapeDtypeStruct((n_batch, seq + 1, heads, HEAD_DIM), bf16),
             ),
             in_specs=[
-                row((group_n, tok, cols), (0, 0, 0)),
-                row((tok, width), (0, 0)),
+                pl.BlockSpec((1, group_n, tok, cols), lambda b: (jnp.maximum(b, late), 0, 0, 0)),
+                pl.BlockSpec((1, tok, width), lambda b: (jnp.maximum(b, late), 0, 0)),
+                any_spec,
                 vm_spec,
-                vm_spec,
-                pl.BlockSpec((1, pair, seq, cols), lambda b: (1, b, 0, 0)),
-                pl.BlockSpec((1, pair, seq, cols), lambda b: (2, b, 0, 0)),
+                pl.BlockSpec((1, tok, width), lambda b: (jnp.minimum(b, late - 1), 0, 0)),
+                pl.BlockSpec((1, 1, seq, cols), lambda b: (1, b, 0, 0)),
+                pl.BlockSpec((1, 1, seq, cols), lambda b: (2, b, 0, 0)),
                 row((1, cols), (0, 0)),
                 row((1, cols), (0, 0)),
             ],
             out_specs=(row((tok, width), (0, 0)), row((seq + 1, heads, HEAD_DIM), (0, 0, 0)), row((seq + 1, heads, HEAD_DIM), (0, 0, 0))),
-            scratch_shapes=[pltpu.VMEM((pair * tok, width), f32)],
+            scratch_shapes=[pltpu.VMEM((width, width), bf16), pltpu.VMEM((tok, width), f32), dma],
             compiler_params=pltpu.CompilerParams(vmem_limit_bytes=VMEM_BYTES),
-        )(o_all, prompt_blk, w_o, post, qkv, qkv, k_new[:, None], v_new[:, None])
+        )(o_all, prompt_blk, w_o, post, out_early, qkv, qkv, k_new, v_new)
         return out_p, k_cache, v_cache, out_d
 
     replicated = P()

time: 404 us -> 383 us (0.948)
  Pallas kernels: 396 us -> 380 us
    pallas_call x1, Pallas kernels: 32.9 us -> 24.7 us  [device_step(): pl.pallas_call(output_kernel, grid=(n_batch,), out_shape=(jax.ShapeDtypeS...]
    pallas_call x1, Pallas kernels: 363 us -> 355 us  [device_step(): pl.pallas_call(functools.partial(exchange_kernel, group_n), out_shape=(ja...]
where the time goes in v3:
time: 383 us; the launch traced here: 382 us
  Pallas kernels  380 us (99%)
    pallas_call x1, Pallas kernels, device_step(): pl.pallas_call(functools.partial(exchange_kernel, group_n), out_shape=(ja...  355 us
    pallas_call x1, Pallas kernels, device_step(): pl.pallas_call(output_kernel, grid=(n_batch,), out_shape=(jax.ShapeDtypeS...  24.7 us

profile of v3, /device:TPU:81, one launch (start us, length us, event | category | flops | bytes accessed | tf_op | source)
XLA Modules:
  0.0 382.1 jit_solution(1009461042242976228)
XLA Ops:
  0.7 1.3 fusion
  1.9 354.9 %shard_map.120 = (bf16[3,8,2048,256]{3,2,1,0:T(8,128)(2,1)}, bf16[8,8,256,256]{3,2,1,0:T(8,128)(2,1)}, bf16[8,2,2,2,256,256]{5,4,3,2,1,0:T(8,128)(2,1)}, bf16[8,...) custom-call(bf16[8,256,2048]{2,1,0:T(8,128)(2,1)} %x_ref.1, ...), custom_call_target="tpu_custom_call" | custom-call | tf_op jit(solution)/shard_map/pallas_call | solution.py:521
  356.8 0.0 copy-start
  356.8 24.7 %shard_map.121 = (bf16[8,256,2048]{2,1,0:T(8,128)(2,1)}, bf16[8,2049,2,128]{3,2,1,0:T(2,128)(2,1)}, bf16[8,2049,2,128]{3,2,1,0:T(2,128)(2,1)}) custom-call(bf16[8,8,256,256]{3,2,1,0:T(8,128)(2,1)} %get-tuple-element.13.o_ref, bf16[8,256,2048]{2,1,0:T(8,128)(2,1)} %x_ref.1, bf16[2048,2048]{1,0:T(8,128)(2,1)} %wo_hbm.3, f32[1,2048]{1,0:T(1,128)} %bitcast.4, ...), custom_call_target="tpu_custom_call" | custom-call | tf_op jit(solution)/shard_map/pallas_call | solution.py:565
  381.5 0.0 copy-done
  381.5 0.6 copy.14
  (2 shorter events, 0.0 us)
Async XLA Ops:
  356.8 24.7 %copy-start = (bf16[8,2048]{1,0:T(8,128)(2,1)S(1)}, bf16[8,2048]{1,0:T(8,128)(2,1)}, u32[]{:S(2)}) copy-start(bf16[8,2048]{1,0:T(8,128)(2,1)} %get-tuple-element.33) | copy-start | bytes 98308

commit v4 on v3

--- a/solution.py
+++ b/solution.py
@@ -13,28 +13,25 @@
 CORES = 2
 LOG2E = 1.4426950408889634
 SLOTS = 3
-LATE = 2
 COL_TILE = 512
 VMEM_BYTES = 66_000_000
 
 
-def rope_tables(positions):
-    lane = jnp.arange(HEAD_DIM) % (HEAD_DIM // 2)
-    inv_freq = ROPE_THETA ** (-(2 * lane).astype(jnp.float32) / HEAD_DIM)
-    angles = positions.astype(jnp.float32)[:, None] * inv_freq[None, :]
-    sign = jnp.where(jnp.arange(HEAD_DIM) < HEAD_DIM // 2, -1.0, 1.0)
-    return jnp.cos(angles), jnp.sin(angles) * sign[None, :]
+def rope_rows():
+    lane = jnp.arange(HEAD_DIM)
+    inv_freq = ROPE_THETA ** (-(2 * (lane % (HEAD_DIM // 2))).astype(jnp.float32) / HEAD_DIM)
+    return inv_freq[None], jnp.where(lane < HEAD_DIM // 2, -1.0, 1.0)[None]
 
 
 def rotate(values, cos_t, sin_t):
     return values * cos_t + pltpu.roll(values, HEAD_DIM // 2, 1) * sin_t
 
 
-def exchange_kernel(group_n, x_hbm, wq_hbm, wk_hbm, wv_hbm, wo_hbm, qgain_ref, kgain_ref, post_ref, cos_ref, sin_ref, new_ref,
+def exchange_kernel(group_n, x_hbm, wq_hbm, wk_hbm, wv_hbm, wo_hbm, qgain_ref, kgain_ref, post_ref, freq_ref, sign_ref, new_ref,
                     qkv_ref, o_ref, relkv_ref, relq_ref, relo_ref, kvp_ref, outp_ref, knew_ref, vnew_ref, outd_ref,
-                    w_vm, x_vm, raw_vm, ssq_vm, stage_vm, qkv_vm, ostage_vm, kvp_vm, olocal_vm, wo_vm, oin_vm, xo_vm, outv_vm, qnew_vm, knew_vm, vnew_vm, deco_vm, decp_vm,
+                    w_vm, x_vm, raw_vm, ssq_vm, stage_vm, qkv_vm, ostage_vm, kvp_vm, olocal_vm, wo_vm, oin_vm, xo_vm, outv_vm, qnew_vm, knew_vm, vnew_vm, deco_vm, decp_vm, cos_vm, sin_vm,
                     w_sem, x_sem, wo_sem, send_sem, recvkv_sem, recvq_sem, relkv_sem, relq_sem, relo_sem, fwdkv_sem, fwdq_sem, fwdo_sem,
-                    load_sem, osend_sem, orecv_sem, kvps_sem, kvpr_sem, kvpl_sem, olocal_sem, oin_sem, xo_sem, outv_sem, decs_sem, decr_sem):
+                    load_sem, osend_sem, oown_sem, orecv_sem, kvps_sem, kvpr_sem, kvpl_sem, olocal_sem, oin_sem, xo_sem, outv_sem, decs_sem, decr_sem):
     n_batch, tok, width = x_hbm.shape
     cols = width // group_n
     heads = cols // HEAD_DIM
@@ -67,21 +64,27 @@
             def _():
                 use(n)
 
-    def w_copy(j):
-        return pltpu.make_async_copy(w_hbm[j], w_vm.at[j], w_sem.at[j])
+    def w_copy(j, n):
+        at = pl.ds(n * COL_TILE, COL_TILE)
+        return pltpu.make_async_copy(w_hbm[j].at[:, at], w_vm.at[j, :, at], w_sem.at[j, n])
 
     def x_copy(t):
         return pltpu.make_async_copy(x_hbm.at[t], x_vm.at[lax.rem(t, 2)], x_sem.at[lax.rem(t, 2)])
 
     x_copy(0).start()
     for j in (2, 1, 0):
-        w_copy(j).start()
+        for n in range(width // COL_TILE):
+            w_copy(j, n).start()
     wo_copy = pltpu.make_async_copy(wo_hbm, wo_vm, wo_sem)
     wo_copy.start()
 
     barrier = pltpu.get_barrier_semaphore()
     for step in range(1, group_n):
         pl.semaphore_signal(barrier, inc=1, device_id={"sp": lax.rem(me + step, group_n)}, device_id_type=pl.DeviceIdType.MESH)
+    place = lax.broadcasted_iota(jnp.int32, cos_vm.shape, 0)
+    angles = jnp.where(place < tok, me * tok + place, group_n * tok).astype(jnp.float32) * freq_ref[...]
+    cos_vm[...] = jnp.cos(angles)
+    sin_vm[...] = jnp.sin(angles) * sign_ref[...]
     pl.semaphore_wait(barrier, group_n - 1)
 
     def send_tensor(t, slot, j):
@@ -132,14 +135,14 @@
 
         x_slot = lax.rem(t, 2)
         for j in (2, 1, 0):
-            @pl.when(t == 0)
-            def _():
-                w_copy(j).wait()
-
             if j < 2:
                 ssq_vm[...] = jnp.zeros_like(ssq_vm)
 
             def col_tile(n, _):
+                @pl.when(t == 0)
+                def _():
+                    w_copy(j, n).wait()
+
                 at = pl.ds(pl.multiple_of(n * COL_TILE, COL_TILE), COL_TILE)
                 acc = jnp.dot(x_vm[x_slot], w_vm[j, :, at], preferred_element_type=jnp.float32)
                 if j < 2:
@@ -159,7 +162,7 @@
                     for h in range(heads):
                         at = pl.ds(pl.multiple_of(n * cols + h * HEAD_DIM, HEAD_DIM), HEAD_DIM)
                         normed = raw_vm[:, at] * inv * gains[j][:, at]
-                        stage_vm[slot, j, n, :, h * HEAD_DIM:(h + 1) * HEAD_DIM] = rotate(normed, cos_ref[:tok], sin_ref[:tok]).astype(jnp.bfloat16)
+                        stage_vm[slot, j, n, :, h * HEAD_DIM:(h + 1) * HEAD_DIM] = rotate(normed, cos_vm[:tok], sin_vm[:tok]).astype(jnp.bfloat16)
                     return 0
 
                 lax.fori_loop(0, group_n, group_tile, 0)
@@ -201,7 +204,7 @@
             def _():
                 drain(relo_ref.at[b, way, :, at], relo_sem.at[b, way])
                 for c in range(CORES):
-                    remote(relo_ref.at[b, way, c, at], o_ref.at[b, source_dev, at], fwdo_sem.at[way], orecv_sem.at[b], to * CORES + c).start()
+                    remote(relo_ref.at[b, way, c, at], o_ref.at[b, source_dev, at], fwdo_sem.at[way], orecv(b, source_dev), to * CORES + c).start()
 
         relay_ways(way_o)
 
@@ -220,6 +223,9 @@
 
         relay_ways(way_all)
 
+    def orecv(b, source_dev):
+        return orecv_sem.at[b + source_dev * (b // (n_batch - 1))]
+
     def send_o(b, slot, dev):
         src = ostage_vm.at[slot, pl.ds(dev * tok, tok)]
         c = dev % CORES
@@ -227,11 +233,11 @@
 
         @pl.when(dev == me)
         def _():
-            pltpu.make_async_copy(src, o_ref.at[b, me], osend_sem.at[b]).start()
+            pltpu.make_async_copy(src, o_ref.at[b, me], oown_sem.at[b]).start()
 
         @pl.when(jnp.logical_and(dev != me, away != 2))
         def _():
-            remote(src, o_ref.at[b, me], osend_sem.at[b], orecv_sem.at[b], dev).start()
+            remote(src, o_ref.at[b, me], osend_sem.at[b], orecv(b, me), dev).start()
 
         @pl.when(away == 2)
         def _():
@@ -243,8 +249,18 @@
 
             with_split(chip, two_hops)
 
-    def drain_o_sends(b):
-        drain(ostage_vm.at[lax.rem(b, 2), pl.ds(first_rows, (group_n - CORES) * tok)], osend_sem.at[b])
+    def drain_o_sends(b, own):
+        slot = lax.rem(b, 2)
+
+        @pl.when(on_first)
+        def _():
+            drain(ostage_vm.at[slot, pl.ds(0, (group_n - CORES) * tok)], osend_sem.at[b])
+
+        @pl.when(jnp.logical_not(on_first))
+        def _():
+            drain(ostage_vm.at[slot, pl.ds(0, (group_n - CORES - 1) * tok)], osend_sem.at[b])
+            if own:
+                drain(ostage_vm.at[slot, pl.ds(0, tok)], oown_sem.at[b])
 
     def new_row():
         def full(j):
@@ -263,7 +279,7 @@
             normed = raw * inv * gains[j][:, own]
             for h in range(heads):
                 at = slice(h * HEAD_DIM, (h + 1) * HEAD_DIM)
-                to[:, at] = rotate(normed[:, at], cos_ref[tok:tok + 1], sin_ref[tok:tok + 1]).astype(jnp.bfloat16)
+                to[:, at] = rotate(normed[:, at], cos_vm[tok:tok + 1], sin_vm[tok:tok + 1]).astype(jnp.bfloat16)
         vnew_vm[...] = jnp.dot(new_ref[...], w_vm[2, :, own], preferred_element_type=jnp.float32).astype(jnp.bfloat16)
         for b in range(n_batch):
             knew_ref[b] = knew_vm[b:b + 1]
@@ -328,7 +344,7 @@
 
         @pl.when(b >= 2)
         def _():
-            drain_o_sends(b - 2)
+            drain_o_sends(b - 2, True)
 
         load_kv.wait()
         load_q.wait()
@@ -357,13 +373,28 @@
             out = out + (last * inv).astype(jnp.bfloat16).astype(jnp.float32) * vnew_vm[:, at].astype(jnp.float32)
             deco_vm[:, at] = jnp.where(mine, out, deco_vm[:, at])
 
+    def finish_rows(b, load_x):
+        inv = lax.rsqrt(jnp.sum(ssq_vm[...], axis=1, keepdims=True) / width + NORM_EPS)
+        load_x.wait()
+
+        def out_tile(n, _):
+            at = pl.ds(pl.multiple_of(n * cols, cols), cols)
+            outv_vm[:, at] = (xo_vm[:, at].astype(jnp.float32) + raw_vm[:, at] * inv * post_ref[:, at]).astype(jnp.bfloat16)
+            return 0
+
+        lax.fori_loop(0, group_n, out_tile, 0)
+        pltpu.make_async_copy(outv_vm, outp_ref.at[b], outv_sem).start()
+
+    def o_copy(b, g, k):
+        return pltpu.make_async_copy(o_ref.at[b, g], oin_vm.at[:, pl.ds(pl.multiple_of(g * cols, cols), cols)], oin_sem.at[k])
+
     def output_rows(b):
         @pl.when(jnp.logical_not(on_first))
         def _():
             drain(o_ref.at[b, pl.ds(0, group_n - 1)], orecv_sem.at[b])
 
         for g in range(group_n):
-            pltpu.make_async_copy(o_ref.at[b, g], oin_vm.at[:, pl.ds(g * cols, cols)], oin_sem).start()
+            o_copy(b, g, 0).start()
         load_x = pltpu.make_async_copy(x_hbm.at[b], xo_vm, xo_sem)
         load_x.start()
 
@@ -376,7 +407,7 @@
             wo_copy.wait()
 
         ssq_vm[...] = jnp.zeros_like(ssq_vm)
-        drain(oin_vm, oin_sem)
+        drain(oin_vm, oin_sem.at[0])
 
         def col_tile(n, _):
             at = pl.ds(pl.multiple_of(n * COL_TILE, COL_TILE), COL_TILE)
@@ -387,16 +418,48 @@
             return 0
 
         lax.fori_loop(0, width // COL_TILE, col_tile, 0)
-        inv = lax.rsqrt(jnp.sum(ssq_vm[...], axis=1, keepdims=True) / width + NORM_EPS)
-        load_x.wait()
-
-        def out_tile(n, _):
-            at = pl.ds(pl.multiple_of(n * cols, cols), cols)
-            outv_vm[:, at] = (xo_vm[:, at].astype(jnp.float32) + raw_vm[:, at] * inv * post_ref[:, at]).astype(jnp.bfloat16)
-            return 0
-
-        lax.fori_loop(0, group_n, out_tile, 0)
-        pltpu.make_async_copy(outv_vm, outp_ref.at[b], outv_sem).start()
+        finish_rows(b, load_x)
+
+    def last_rows(b):
+        load_x = pltpu.make_async_copy(x_hbm.at[b], xo_vm, xo_sem)
+        load_x.start()
+
+        @pl.when(on_first)
+        def _():
+            drain(olocal_vm, olocal_sem)
+
+        drain(outv_vm, outv_sem)
+        ssq_vm[...] = jnp.zeros_like(ssq_vm)
+        both = CORES * cols
+        for k, source in enumerate((chip, right, left, far)):
+            if k:
+                @pl.when(jnp.logical_not(on_first))
+                def _():
+                    for c in range(CORES):
+                        drain(o_ref.at[b, source * CORES + c], orecv(b, source * CORES + c))
+            else:
+                @pl.when(jnp.logical_not(on_first))
+                def _():
+                    drain(o_ref.at[b, me], oown_sem.at[b])
+                    drain(o_ref.at[b, partner], orecv(b, partner))
+            for c in range(CORES):
+                o_copy(b, source * CORES + c, k).start()
+            part = pl.ds(pl.multiple_of(source * both, both), both)
+            drain(oin_vm.at[:, part], oin_sem.at[k])
+
+            def col_tile(n, _):
+                at = pl.ds(pl.multiple_of(n * COL_TILE, COL_TILE), COL_TILE)
+                acc = jnp.dot(oin_vm[:, part], wo_vm[part, at], preferred_element_type=jnp.float32)
+                if k:
+                    acc = acc + raw_vm[:, at]
+                raw_vm[:, at] = acc
+                if k == 3:
+                    sq = acc * acc
+                    ssq_vm[...] += sum(sq[:, i * HEAD_DIM:(i + 1) * HEAD_DIM] for i in range(COL_TILE // HEAD_DIM))
+                return 0
+
+            lax.fori_loop(0, width // COL_TILE, col_tile, 0)
+        finish_rows(b, load_x)
 
     def send_part():
         own = pl.ds(pl.multiple_of(me * cols, cols), cols)
@@ -430,15 +493,24 @@
         def _():
             forward(t)
 
-        @pl.when(jnp.logical_and(t >= 3, t < n_batch + 3 - LATE))
+        @pl.when(jnp.logical_and(t >= 3, t < n_batch))
         def _():
             output_rows(t - 3)
 
+        return 0
+
+    def rest(b, _):
+        @pl.when(b == n_batch - 2)
+        def _():
+            drain_o_sends(b, True)
+
+        output_rows(b)
         return 0
 
     lax.fori_loop(0, n_batch + 1, step, 0)
     send_part()
     forward_o(n_batch - 1)
+    lax.fori_loop(n_batch - 3, n_batch - 1, rest, 0)
 
     drain(decp_vm.at[pl.ds(0, group_n - 1)], decs_sem)
     drain(decp_vm.at[pl.ds(0, group_n - 1)], decr_sem)
@@ -448,56 +520,19 @@
     inv = lax.rsqrt(jnp.sum(proj * proj, axis=1, keepdims=True) / width + NORM_EPS)
     outd_ref[...] = (new_ref[...].astype(jnp.float32) + proj * inv * post_ref[...]).astype(jnp.bfloat16)
 
+    last_rows(n_batch - 1)
     for t in range(n_batch - SLOTS, n_batch):
         drain_sends(t)
-    for b in range(n_batch - 2, n_batch):
-        drain_o_sends(b)
+    drain_o_sends(n_batch - 1, False)
     drain_forwards()
-
-    @pl.when(on_first)
-    def _():
-        drain(olocal_vm, olocal_sem)
-
-    @pl.when(jnp.logical_not(on_first))
-    def _():
-        for b in range(n_batch - LATE, n_batch):
-            drain(o_ref.at[b, pl.ds(0, group_n - 1)], orecv_sem.at[b])
-
     drain(outv_vm, outv_sem)
 
 
-def output_kernel(o_ref, x_ref, wo_hbm, post_ref, outp_ref, k_ref, v_ref, knew_ref, vnew_ref, out_ref, kc_ref, vc_ref, wo_vm, raw_vm, wo_sem):
-    _, group_n, tok, cols = o_ref.shape
-    width = group_n * cols
+def output_kernel(outp_ref, k_ref, v_ref, knew_ref, vnew_ref, outd_in_ref, out_ref, kc_ref, vc_ref, outd_ref):
+    out_ref[...] = outp_ref[...]
+    outd_ref[...] = outd_in_ref[...]
+    seq, cols = k_ref.shape[2:]
     heads = cols // HEAD_DIM
-    b, n_batch = pl.program_id(0), pl.num_programs(0)
-    wo_copy = pltpu.make_async_copy(wo_hbm, wo_vm, wo_sem)
-
-    @pl.when(b == 0)
-    def _():
-        wo_copy.start()
-
-    @pl.when(b < n_batch - LATE)
-    def _():
-        out_ref[...] = outp_ref[...]
-
-    @pl.when(b == n_batch - LATE)
-    def _():
-        wo_copy.wait()
-
-    @pl.when(b >= n_batch - LATE)
-    def _():
-        o_all = jnp.concatenate([o_ref[0, g] for g in range(group_n)], axis=1)
-        ssq = jnp.zeros((tok, 1), jnp.float32)
-        for n in range(width // COL_TILE):
-            at = slice(n * COL_TILE, (n + 1) * COL_TILE)
-            acc = jnp.dot(o_all, wo_vm[:, at], preferred_element_type=jnp.float32)
-            raw_vm[:, at] = acc
-            ssq = ssq + jnp.sum(acc * acc, axis=1, keepdims=True)
-        inv = lax.rsqrt(ssq / width + NORM_EPS)
-        out_ref[0] = (x_ref[0].astype(jnp.float32) + raw_vm[...] * inv * post_ref[...]).astype(jnp.bfloat16)
-
-    seq = k_ref.shape[2]
     for src, new, to in ((k_ref, knew_ref, kc_ref), (v_ref, vnew_ref, vc_ref)):
         to[0, :seq] = src[0, 0].reshape(seq, heads, HEAD_DIM)
         to[0, seq:] = new[0].reshape(1, heads, HEAD_DIM)
@@ -512,13 +547,12 @@
         heads = cols // HEAD_DIM
         seq = tok * group_n
         bf16, f32 = jnp.bfloat16, jnp.float32
-        step = jnp.arange(tok + 8)
-        cos_t, sin_t = rope_tables(jnp.where(step < tok, lax.axis_index("sp") * tok + step, seq))
+        freq, sign = rope_rows()
         q_gain, k_gain, post = q_norm_w[None], k_norm_w[None], post_norm_w[None]
         any_spec = pl.BlockSpec(memory_space=pl.ANY)
         vm_spec = pl.BlockSpec(memory_space=pltpu.VMEM)
         dma = pltpu.SemaphoreType.DMA
-        qkv, o_all, _, _, _, _, out_early, k_new, v_new, out_d = pl.pallas_call(
+        qkv, _, _, _, _, _, out_rows, k_new, v_new, out_d = pl.pallas_call(
             functools.partial(exchange_kernel, group_n),
             out_shape=(
                 jax.ShapeDtypeStruct((3, n_batch, seq, cols), bf16),
@@ -527,7 +561,7 @@
                 jax.ShapeDtypeStruct((n_batch, 2, CORES, tok, cols), bf16),
                 jax.ShapeDtypeStruct((n_batch, 2, CORES, tok, cols), bf16),
                 jax.ShapeDtypeStruct((n_batch, 2, group_n, tok, cols), bf16),
-                jax.ShapeDtypeStruct((n_batch - LATE, tok, width), bf16),
+                jax.ShapeDtypeStruct((n_batch, tok, width), bf16),
                 jax.ShapeDtypeStruct((n_batch, 1, cols), bf16),
                 jax.ShapeDtypeStruct((n_batch, 1, cols), bf16),
                 jax.ShapeDtypeStruct((n_batch, width), bf16),
@@ -553,38 +587,38 @@
                 pltpu.VMEM((n_batch, cols), bf16),
                 pltpu.VMEM((n_batch, cols), f32),
                 pltpu.VMEM((group_n, n_batch, width), bf16),
-                dma((3,)), dma((2,)), dma,
+                pltpu.VMEM((tok + 8, HEAD_DIM), f32),
+                pltpu.VMEM((tok + 8, HEAD_DIM), f32),
+                dma((3, width // COL_TILE)), dma((2,)), dma,
                 dma((n_batch,)), dma((n_batch,)), dma((n_batch,)), dma((n_batch, 2)), dma((n_batch, 2)), dma((n_batch, 2)), dma((2,)), dma((2,)), dma((2,)),
-                dma((2,)), dma((n_batch,)), dma((n_batch,)), dma((n_batch,)), dma((n_batch,)), dma, dma, dma, dma, dma, dma, dma,
+                dma((2,)), dma((n_batch,)), dma((n_batch,)), dma((n_batch + group_n,)), dma((n_batch,)), dma((n_batch,)), dma, dma, dma((group_n // CORES,)), dma, dma, dma, dma,
             ],
             compiler_params=pltpu.CompilerParams(collective_id=0, has_side_effects=True, vmem_limit_bytes=VMEM_BYTES),
-        )(prompt_blk, w_q, w_k, w_v, w_o, q_gain, k_gain, post, cos_t, sin_t, new_rows)
+        )(prompt_blk, w_q, w_k, w_v, w_o, q_gain, k_gain, post, freq, sign, new_rows)
 
         row = lambda shape, at: pl.BlockSpec((1,) + shape, lambda b: (b,) + at)
-        late = n_batch - LATE
-        out_p, k_cache, v_cache = pl.pallas_call(
+        whole = pl.BlockSpec((n_batch, width), lambda b: (0, 0))
+        cache = row((seq + 1, heads, HEAD_DIM), (0, 0, 0))
+        out_p, k_cache, v_cache, out_d = pl.pallas_call(
             output_kernel,
             grid=(n_batch,),
             out_shape=(
                 jax.ShapeDtypeStruct((n_batch, tok, width), bf16),
                 jax.ShapeDtypeStruct((n_batch, seq + 1, heads, HEAD_DIM), bf16),
                 jax.ShapeDtypeStruct((n_batch, seq + 1, heads, HEAD_DIM), bf16),
+                jax.ShapeDtypeStruct((n_batch, width), bf16),
             ),
             in_specs=[
-                pl.BlockSpec((1, group_n, tok, cols), lambda b: (jnp.maximum(b, late), 0, 0, 0)),
-                pl.BlockSpec((1, tok, width), lambda b: (jnp.maximum(b, late), 0, 0)),
-                any_spec,
-                vm_spec,
-                pl.BlockSpec((1, tok, width), lambda b: (jnp.minimum(b, late - 1), 0, 0)),
+                row((tok, width), (0, 0)),
                 pl.BlockSpec((1, 1, seq, cols), lambda b: (1, b, 0, 0)),
                 pl.BlockSpec((1, 1, seq, cols), lambda b: (2, b, 0, 0)),
                 row((1, cols), (0, 0)),
                 row((1, cols), (0, 0)),
+                whole,
             ],
-            out_specs=(row((tok, width), (0, 0)), row((seq + 1, heads, HEAD_DIM), (0, 0, 0)), row((seq + 1, heads, HEAD_DIM), (0, 0, 0))),
-            scratch_shapes=[pltpu.VMEM((width, width), bf16), pltpu.VMEM((tok, width), f32), dma],
+            out_specs=(row((tok, width), (0, 0)), cache, cache, whole),
             compiler_params=pltpu.CompilerParams(vmem_limit_bytes=VMEM_BYTES),
-        )(o_all, prompt_blk, w_o, post, out_early, qkv, qkv, k_new, v_new)
+        )(out_rows, qkv, qkv, k_new, v_new, out_d)
         return out_p, k_cache, v_cache, out_d
 
     replicated = P()

time: 383 us -> 389 us (1.016)
  Pallas kernels: 380 us -> 387 us
    pallas_call x1, Pallas kernels: 355 us -> 368 us  [device_step(): pl.pallas_call(functools.partial(exchange_kernel, group_n), out_shape=(ja...]
    pallas_call x1, Pallas kernels: 24.7 us -> 18.5 us  [device_step(): pl.pallas_call(output_kernel, grid=(n_batch,), out_shape=(jax.ShapeDtypeS...]
where the time goes in v4:
time: 389 us; the launch traced here: 388 us
  Pallas kernels  387 us (99%)
    pallas_call x1, Pallas kernels, device_step(): pl.pallas_call(functools.partial(exchange_kernel, group_n), out_shape=(ja...  368 us
    pallas_call x1, Pallas kernels, device_step(): pl.pallas_call(output_kernel, grid=(n_batch,), out_shape=(jax.ShapeDtypeS...  18.5 us

profile of v4, /device:TPU:81, one launch (start us, length us, event | category | flops | bytes accessed | tf_op | source)
XLA Modules:
  0.0 388.0 jit_solution(869357828397667186)
XLA Ops:
  0.6 0.5 compare_select_fusion
  1.2 368.4 %shard_map.120 = (bf16[3,8,2048,256]{3,2,1,0:T(8,128)(2,1)}, bf16[8,8,256,256]{3,2,1,0:T(8,128)(2,1)}, bf16[8,2,2,2,256,256]{5,4,3,2,1,0:T(8,128)(2,1)}, bf16[8,...) custom-call(bf16[8,256,2048]{2,1,0:T(8,128)(2,1)} %x_hbm.1, ...), custom_call_target="tpu_custom_call" | custom-call | tf_op jit(solution)/shard_map/pallas_call | solution.py:555
  369.6 18.5 %shard_map.121 = (bf16[8,256,2048]{2,1,0:T(8,128)(2,1)}, bf16[8,2049,2,128]{3,2,1,0:T(2,128)(2,1)}, bf16[8,2049,2,128]{3,2,1,0:T(2,128)(2,1)}, bf16[8,2048]{1,0:T(8,128)(2,1)}) custom-call(bf16[8,256,2048]{2,1,0:T(8,128)(2,1)} %get-tuple-element.9.outp_ref, bf16[3,8,2048,256]{3,2,1,0:T(8,128)(2,1)} %get-tuple-element.10.k_ref.v_ref, ...), custom_call_target="tpu_custom_call" | custom-call | tf_op jit(solution)/shard_map/pallas_call | solution.py:602

commit v5 on v4

--- a/solution.py
+++ b/solution.py
@@ -64,19 +64,15 @@
             def _():
                 use(n)
 
-    def w_copy(j, n):
-        at = pl.ds(n * COL_TILE, COL_TILE)
-        return pltpu.make_async_copy(w_hbm[j].at[:, at], w_vm.at[j, :, at], w_sem.at[j, n])
+    def w_copy(j):
+        return pltpu.make_async_copy(w_hbm[j], w_vm.at[j], w_sem.at[j])
 
     def x_copy(t):
         return pltpu.make_async_copy(x_hbm.at[t], x_vm.at[lax.rem(t, 2)], x_sem.at[lax.rem(t, 2)])
 
     x_copy(0).start()
-    for j in (2, 1, 0):
-        for n in range(width // COL_TILE):
-            w_copy(j, n).start()
+    w_copy(2).start()
     wo_copy = pltpu.make_async_copy(wo_hbm, wo_vm, wo_sem)
-    wo_copy.start()
 
     barrier = pltpu.get_barrier_semaphore()
     for step in range(1, group_n):
@@ -135,14 +131,15 @@
 
         x_slot = lax.rem(t, 2)
         for j in (2, 1, 0):
+            @pl.when(t == 0)
+            def _():
+                w_copy(j).wait()
+                (w_copy(j - 1) if j else wo_copy).start()
+
             if j < 2:
                 ssq_vm[...] = jnp.zeros_like(ssq_vm)
 
             def col_tile(n, _):
-                @pl.when(t == 0)
-                def _():
-                    w_copy(j, n).wait()
-
                 at = pl.ds(pl.multiple_of(n * COL_TILE, COL_TILE), COL_TILE)
                 acc = jnp.dot(x_vm[x_slot], w_vm[j, :, at], preferred_element_type=jnp.float32)
                 if j < 2:
@@ -249,7 +246,7 @@
 
             with_split(chip, two_hops)
 
-    def drain_o_sends(b, own):
+    def drain_o_sends(b):
         slot = lax.rem(b, 2)
 
         @pl.when(on_first)
@@ -259,8 +256,6 @@
         @pl.when(jnp.logical_not(on_first))
         def _():
             drain(ostage_vm.at[slot, pl.ds(0, (group_n - CORES - 1) * tok)], osend_sem.at[b])
-            if own:
-                drain(ostage_vm.at[slot, pl.ds(0, tok)], oown_sem.at[b])
 
     def new_row():
         def full(j):
@@ -344,7 +339,11 @@
 
         @pl.when(b >= 2)
         def _():
-            drain_o_sends(b - 2, True)
+            drain_o_sends(b - 2)
+
+        @pl.when(jnp.logical_and(b >= 1, jnp.logical_not(on_first)))
+        def _():
+            drain(o_ref.at[b - 1, me], oown_sem.at[b - 1])
 
         load_kv.wait()
         load_q.wait()
@@ -481,9 +480,9 @@
         def _():
             forward_o(t - 2)
 
-        @pl.when(jnp.logical_and(on_first, t >= 1))
-        def _():
-            attend_first(t - 1)
+        @pl.when(t == n_batch)
+        def _():
+            output_rows(t - 3)
 
         @pl.when(t >= 1)
         def _():
@@ -493,24 +492,20 @@
         def _():
             forward(t)
 
+        @pl.when(jnp.logical_and(on_first, t < n_batch))
+        def _():
+            attend_first(t)
+
         @pl.when(jnp.logical_and(t >= 3, t < n_batch))
         def _():
             output_rows(t - 3)
 
         return 0
 
-    def rest(b, _):
-        @pl.when(b == n_batch - 2)
-        def _():
-            drain_o_sends(b, True)
-
-        output_rows(b)
-        return 0
-
     lax.fori_loop(0, n_batch + 1, step, 0)
+    forward_o(n_batch - 1)
     send_part()
-    forward_o(n_batch - 1)
-    lax.fori_loop(n_batch - 3, n_batch - 1, rest, 0)
+    output_rows(n_batch - 2)
 
     drain(decp_vm.at[pl.ds(0, group_n - 1)], decs_sem)
     drain(decp_vm.at[pl.ds(0, group_n - 1)], decr_sem)
@@ -523,7 +518,8 @@
     last_rows(n_batch - 1)
     for t in range(n_batch - SLOTS, n_batch):
         drain_sends(t)
-    drain_o_sends(n_batch - 1, False)
+    drain_o_sends(n_batch - 2)
+    drain_o_sends(n_batch - 1)
     drain_forwards()
     drain(outv_vm, outv_sem)
 
@@ -589,7 +585,7 @@
                 pltpu.VMEM((group_n, n_batch, width), bf16),
                 pltpu.VMEM((tok + 8, HEAD_DIM), f32),
                 pltpu.VMEM((tok + 8, HEAD_DIM), f32),
-                dma((3, width // COL_TILE)), dma((2,)), dma,
+                dma((3,)), dma((2,)), dma,
                 dma((n_batch,)), dma((n_batch,)), dma((n_batch,)), dma((n_batch, 2)), dma((n_batch, 2)), dma((n_batch, 2)), dma((2,)), dma((2,)), dma((2,)),
                 dma((2,)), dma((n_batch,)), dma((n_batch,)), dma((n_batch + group_n,)), dma((n_batch,)), dma((n_batch,)), dma, dma, dma((group_n // CORES,)), dma, dma, dma, dma,
             ],

time: 389 us -> 385 us (0.990)
  Pallas kernels: 387 us -> 382 us
    pallas_call x1, Pallas kernels: 368 us -> 364 us  [device_step(): pl.pallas_call(functools.partial(exchange_kernel, group_n), out_shape=(ja...]
where the time goes in v5:
time: 385 us; the launch traced here: 384 us
  Pallas kernels  382 us (99%)
    pallas_call x1, Pallas kernels, device_step(): pl.pallas_call(functools.partial(exchange_kernel, group_n), out_shape=(ja...  364 us
    pallas_call x1, Pallas kernels, device_step(): pl.pallas_call(output_kernel, grid=(n_batch,), out_shape=(jax.ShapeDtypeS...  18.5 us

profile of v5, /device:TPU:81, one launch (start us, length us, event | category | flops | bytes accessed | tf_op | source)
XLA Modules:
  0.0 383.6 jit_solution(9905095376636075900)
XLA Ops:
  0.6 0.5 compare_select_fusion
  1.2 364.0 %shard_map.120 = (bf16[3,8,2048,256]{3,2,1,0:T(8,128)(2,1)}, bf16[8,8,256,256]{3,2,1,0:T(8,128)(2,1)}, bf16[8,2,2,2,256,256]{5,4,3,2,1,0:T(8,128)(2,1)}, bf16[8,...) custom-call(bf16[8,256,2048]{2,1,0:T(8,128)(2,1)} %x_hbm.1, ...), custom_call_target="tpu_custom_call" | custom-call | tf_op jit(solution)/shard_map/pallas_call | solution.py:551
  365.1 18.5 %shard_map.121 = (bf16[8,256,2048]{2,1,0:T(8,128)(2,1)}, bf16[8,2049,2,128]{3,2,1,0:T(2,128)(2,1)}, bf16[8,2049,2,128]{3,2,1,0:T(2,128)(2,1)}, bf16[8,2048]{1,0:T(8,128)(2,1)}) custom-call(bf16[8,256,2048]{2,1,0:T(8,128)(2,1)} %get-tuple-element.9.outp_ref, bf16[3,8,2048,256]{3,2,1,0:T(8,128)(2,1)} %get-tuple-element.10.k_ref.v_ref, ...), custom_call_target="tpu_custom_call" | custom-call | tf_op jit(solution)/shard_map/pallas_call | solution.py:598

commit v6 on v3

--- a/solution.py
+++ b/solution.py
@@ -18,23 +18,21 @@
 VMEM_BYTES = 66_000_000
 
 
-def rope_tables(positions):
-    lane = jnp.arange(HEAD_DIM) % (HEAD_DIM // 2)
-    inv_freq = ROPE_THETA ** (-(2 * lane).astype(jnp.float32) / HEAD_DIM)
-    angles = positions.astype(jnp.float32)[:, None] * inv_freq[None, :]
-    sign = jnp.where(jnp.arange(HEAD_DIM) < HEAD_DIM // 2, -1.0, 1.0)
-    return jnp.cos(angles), jnp.sin(angles) * sign[None, :]
+def rope_rows():
+    lane = jnp.arange(HEAD_DIM)
+    inv_freq = ROPE_THETA ** (-(2 * (lane % (HEAD_DIM // 2))).astype(jnp.float32) / HEAD_DIM)
+    return inv_freq[None], jnp.where(lane < HEAD_DIM // 2, -1.0, 1.0)[None]
 
 
 def rotate(values, cos_t, sin_t):
     return values * cos_t + pltpu.roll(values, HEAD_DIM // 2, 1) * sin_t
 
 
-def exchange_kernel(group_n, x_hbm, wq_hbm, wk_hbm, wv_hbm, wo_hbm, qgain_ref, kgain_ref, post_ref, cos_ref, sin_ref, new_ref,
+def exchange_kernel(group_n, x_hbm, wq_hbm, wk_hbm, wv_hbm, wo_hbm, qgain_ref, kgain_ref, post_ref, freq_ref, sign_ref, new_ref,
                     qkv_ref, o_ref, relkv_ref, relq_ref, relo_ref, kvp_ref, outp_ref, knew_ref, vnew_ref, outd_ref,
-                    w_vm, x_vm, raw_vm, ssq_vm, stage_vm, qkv_vm, ostage_vm, kvp_vm, olocal_vm, wo_vm, oin_vm, xo_vm, outv_vm, qnew_vm, knew_vm, vnew_vm, deco_vm, decp_vm,
+                    w_vm, x_vm, raw_vm, ssq_vm, stage_vm, qkv_vm, ostage_vm, kvp_vm, olocal_vm, wo_vm, oin_vm, xo_vm, outv_vm, qnew_vm, knew_vm, vnew_vm, deco_vm, decp_vm, cos_vm, sin_vm,
                     w_sem, x_sem, wo_sem, send_sem, recvkv_sem, recvq_sem, relkv_sem, relq_sem, relo_sem, fwdkv_sem, fwdq_sem, fwdo_sem,
-                    load_sem, osend_sem, orecv_sem, kvps_sem, kvpr_sem, kvpl_sem, olocal_sem, oin_sem, xo_sem, outv_sem, decs_sem, decr_sem):
+                    load_sem, osend_sem, oown_sem, orecv_sem, kvps_sem, kvpr_sem, kvpl_sem, olocal_sem, oin_sem, xo_sem, outv_sem, decs_sem, decr_sem):
     n_batch, tok, width = x_hbm.shape
     cols = width // group_n
     heads = cols // HEAD_DIM
@@ -74,14 +72,17 @@
         return pltpu.make_async_copy(x_hbm.at[t], x_vm.at[lax.rem(t, 2)], x_sem.at[lax.rem(t, 2)])
 
     x_copy(0).start()
-    for j in (2, 1, 0):
-        w_copy(j).start()
+    w_copy(2).start()
+    w_copy(1).start()
     wo_copy = pltpu.make_async_copy(wo_hbm, wo_vm, wo_sem)
-    wo_copy.start()
 
     barrier = pltpu.get_barrier_semaphore()
     for step in range(1, group_n):
         pl.semaphore_signal(barrier, inc=1, device_id={"sp": lax.rem(me + step, group_n)}, device_id_type=pl.DeviceIdType.MESH)
+    place = lax.broadcasted_iota(jnp.int32, cos_vm.shape, 0)
+    angles = jnp.where(place < tok, me * tok + place, group_n * tok).astype(jnp.float32) * freq_ref[...]
+    cos_vm[...] = jnp.cos(angles)
+    sin_vm[...] = jnp.sin(angles) * sign_ref[...]
     pl.semaphore_wait(barrier, group_n - 1)
 
     def send_tensor(t, slot, j):
@@ -135,6 +136,8 @@
             @pl.when(t == 0)
             def _():
                 w_copy(j).wait()
+                if j != 1:
+                    (w_copy(0) if j else wo_copy).start()
 
             if j < 2:
                 ssq_vm[...] = jnp.zeros_like(ssq_vm)
@@ -159,7 +162,7 @@
                     for h in range(heads):
                         at = pl.ds(pl.multiple_of(n * cols + h * HEAD_DIM, HEAD_DIM), HEAD_DIM)
                         normed = raw_vm[:, at] * inv * gains[j][:, at]
-                        stage_vm[slot, j, n, :, h * HEAD_DIM:(h + 1) * HEAD_DIM] = rotate(normed, cos_ref[:tok], sin_ref[:tok]).astype(jnp.bfloat16)
+                        stage_vm[slot, j, n, :, h * HEAD_DIM:(h + 1) * HEAD_DIM] = rotate(normed, cos_vm[:tok], sin_vm[:tok]).astype(jnp.bfloat16)
                     return 0
 
                 lax.fori_loop(0, group_n, group_tile, 0)
@@ -227,7 +230,7 @@
 
         @pl.when(dev == me)
         def _():
-            pltpu.make_async_copy(src, o_ref.at[b, me], osend_sem.at[b]).start()
+            pltpu.make_async_copy(src, o_ref.at[b, me], oown_sem.at[b]).start()
 
         @pl.when(jnp.logical_and(dev != me, away != 2))
         def _():
@@ -244,7 +247,15 @@
             with_split(chip, two_hops)
 
     def drain_o_sends(b):
-        drain(ostage_vm.at[lax.rem(b, 2), pl.ds(first_rows, (group_n - CORES) * tok)], osend_sem.at[b])
+        slot = lax.rem(b, 2)
+
+        @pl.when(on_first)
+        def _():
+            drain(ostage_vm.at[slot, pl.ds(0, (group_n - CORES) * tok)], osend_sem.at[b])
+
+        @pl.when(jnp.logical_not(on_first))
+        def _():
+            drain(ostage_vm.at[slot, pl.ds(0, (group_n - CORES - 1) * tok)], osend_sem.at[b])
 
     def new_row():
         def full(j):
@@ -263,7 +274,7 @@
             normed = raw * inv * gains[j][:, own]
             for h in range(heads):
                 at = slice(h * HEAD_DIM, (h + 1) * HEAD_DIM)
-                to[:, at] = rotate(normed[:, at], cos_ref[tok:tok + 1], sin_ref[tok:tok + 1]).astype(jnp.bfloat16)
+                to[:, at] = rotate(normed[:, at], cos_vm[tok:tok + 1], sin_vm[tok:tok + 1]).astype(jnp.bfloat16)
         vnew_vm[...] = jnp.dot(new_ref[...], w_vm[2, :, own], preferred_element_type=jnp.float32).astype(jnp.bfloat16)
         for b in range(n_batch):
             knew_ref[b] = knew_vm[b:b + 1]
@@ -330,6 +341,10 @@
         def _():
             drain_o_sends(b - 2)
 
+        @pl.when(jnp.logical_and(b >= 1, jnp.logical_not(on_first)))
+        def _():
+            drain(o_ref.at[b - 1, me], oown_sem.at[b - 1])
+
         load_kv.wait()
         load_q.wait()
         for blk in range(CORES, group_n):
@@ -357,13 +372,28 @@
             out = out + (last * inv).astype(jnp.bfloat16).astype(jnp.float32) * vnew_vm[:, at].astype(jnp.float32)
             deco_vm[:, at] = jnp.where(mine, out, deco_vm[:, at])
 
+    def finish_rows(b, load_x):
+        inv = lax.rsqrt(jnp.sum(ssq_vm[...], axis=1, keepdims=True) / width + NORM_EPS)
+        load_x.wait()
+
+        def out_tile(n, _):
+            at = pl.ds(pl.multiple_of(n * cols, cols), cols)
+            outv_vm[:, at] = (xo_vm[:, at].astype(jnp.float32) + raw_vm[:, at] * inv * post_ref[:, at]).astype(jnp.bfloat16)
+            return 0
+
+        lax.fori_loop(0, group_n, out_tile, 0)
+        pltpu.make_async_copy(outv_vm, outp_ref.at[b], outv_sem).start()
+
+    def o_copy(b, g):
+        return pltpu.make_async_copy(o_ref.at[b, g], oin_vm.at[:, pl.ds(pl.multiple_of(g * cols, cols), cols)], oin_sem)
+
     def output_rows(b):
         @pl.when(jnp.logical_not(on_first))
         def _():
             drain(o_ref.at[b, pl.ds(0, group_n - 1)], orecv_sem.at[b])
 
         for g in range(group_n):
-            pltpu.make_async_copy(o_ref.at[b, g], oin_vm.at[:, pl.ds(g * cols, cols)], oin_sem).start()
+            o_copy(b, g).start()
         load_x = pltpu.make_async_copy(x_hbm.at[b], xo_vm, xo_sem)
         load_x.start()
 
@@ -387,16 +417,7 @@
             return 0
 
         lax.fori_loop(0, width // COL_TILE, col_tile, 0)
-        inv = lax.rsqrt(jnp.sum(ssq_vm[...], axis=1, keepdims=True) / width + NORM_EPS)
-        load_x.wait()
-
-        def out_tile(n, _):
-            at = pl.ds(pl.multiple_of(n * cols, cols), cols)
-            outv_vm[:, at] = (xo_vm[:, at].astype(jnp.float32) + raw_vm[:, at] * inv * post_ref[:, at]).astype(jnp.bfloat16)
-            return 0
-
-        lax.fori_loop(0, group_n, out_tile, 0)
-        pltpu.make_async_copy(outv_vm, outp_ref.at[b], outv_sem).start()
+        finish_rows(b, load_x)
 
     def send_part():
         own = pl.ds(pl.multiple_of(me * cols, cols), cols)
@@ -430,6 +451,11 @@
         def _():
             forward(t)
 
+        @pl.when(t == n_batch)
+        def _():
+            send_part()
+            forward_o(n_batch - 1)
+
         @pl.when(jnp.logical_and(t >= 3, t < n_batch + 3 - LATE))
         def _():
             output_rows(t - 3)
@@ -437,8 +463,6 @@
         return 0
 
     lax.fori_loop(0, n_batch + 1, step, 0)
-    send_part()
-    forward_o(n_batch - 1)
 
     drain(decp_vm.at[pl.ds(0, group_n - 1)], decs_sem)
     drain(decp_vm.at[pl.ds(0, group_n - 1)], decr_sem)
@@ -450,8 +474,8 @@
 
     for t in range(n_batch - SLOTS, n_batch):
         drain_sends(t)
-    for b in range(n_batch - 2, n_batch):
-        drain_o_sends(b)
+    drain_o_sends(n_batch - 2)
+    drain_o_sends(n_batch - 1)
     drain_forwards()
 
     @pl.when(on_first)
@@ -460,13 +484,14 @@
 
     @pl.when(jnp.logical_not(on_first))
     def _():
+        drain(o_ref.at[n_batch - 1, me], oown_sem.at[n_batch - 1])
         for b in range(n_batch - LATE, n_batch):
             drain(o_ref.at[b, pl.ds(0, group_n - 1)], orecv_sem.at[b])
 
     drain(outv_vm, outv_sem)
 
 
-def output_kernel(o_ref, x_ref, wo_hbm, post_ref, outp_ref, k_ref, v_ref, knew_ref, vnew_ref, out_ref, kc_ref, vc_ref, wo_vm, raw_vm, wo_sem):
+def output_kernel(o_ref, x_ref, wo_hbm, post_ref, outp_ref, k_ref, v_ref, knew_ref, vnew_ref, outd_in_ref, out_ref, kc_ref, vc_ref, outd_ref, wo_vm, raw_vm, wo_sem):
     _, group_n, tok, cols = o_ref.shape
     width = group_n * cols
     heads = cols // HEAD_DIM
@@ -497,6 +522,7 @@
         inv = lax.rsqrt(ssq / width + NORM_EPS)
         out_ref[0] = (x_ref[0].astype(jnp.float32) + raw_vm[...] * inv * post_ref[...]).astype(jnp.bfloat16)
 
+    outd_ref[...] = outd_in_ref[...]
     seq = k_ref.shape[2]
     for src, new, to in ((k_ref, knew_ref, kc_ref), (v_ref, vnew_ref, vc_ref)):
         to[0, :seq] = src[0, 0].reshape(seq, heads, HEAD_DIM)
@@ -512,8 +538,7 @@
         heads = cols // HEAD_DIM
         seq = tok * group_n
         bf16, f32 = jnp.bfloat16, jnp.float32
-        step = jnp.arange(tok + 8)
-        cos_t, sin_t = rope_tables(jnp.where(step < tok, lax.axis_index("sp") * tok + step, seq))
+        freq, sign = rope_rows()
         q_gain, k_gain, post = q_norm_w[None], k_norm_w[None], post_norm_w[None]
         any_spec = pl.BlockSpec(memory_space=pl.ANY)
         vm_spec = pl.BlockSpec(memory_space=pltpu.VMEM)
@@ -553,22 +578,27 @@
                 pltpu.VMEM((n_batch, cols), bf16),
                 pltpu.VMEM((n_batch, cols), f32),
                 pltpu.VMEM((group_n, n_batch, width), bf16),
+                pltpu.VMEM((tok + 8, HEAD_DIM), f32),
+                pltpu.VMEM((tok + 8, HEAD_DIM), f32),
                 dma((3,)), dma((2,)), dma,
                 dma((n_batch,)), dma((n_batch,)), dma((n_batch,)), dma((n_batch, 2)), dma((n_batch, 2)), dma((n_batch, 2)), dma((2,)), dma((2,)), dma((2,)),
-                dma((2,)), dma((n_batch,)), dma((n_batch,)), dma((n_batch,)), dma((n_batch,)), dma, dma, dma, dma, dma, dma, dma,
+                dma((2,)), dma((n_batch,)), dma((n_batch,)), dma((n_batch,)), dma((n_batch,)), dma((n_batch,)), dma, dma, dma, dma, dma, dma, dma,
             ],
             compiler_params=pltpu.CompilerParams(collective_id=0, has_side_effects=True, vmem_limit_bytes=VMEM_BYTES),
-        )(prompt_blk, w_q, w_k, w_v, w_o, q_gain, k_gain, post, cos_t, sin_t, new_rows)
+        )(prompt_blk, w_q, w_k, w_v, w_o, q_gain, k_gain, post, freq, sign, new_rows)
 
         row = lambda shape, at: pl.BlockSpec((1,) + shape, lambda b: (b,) + at)
         late = n_batch - LATE
-        out_p, k_cache, v_cache = pl.pallas_call(
+        whole = pl.BlockSpec((n_batch, width), lambda b: (0, 0))
+        cache = row((seq + 1, heads, HEAD_DIM), (0, 0, 0))
+        out_p, k_cache, v_cache, out_d = pl.pallas_call(
             output_kernel,
             grid=(n_batch,),
             out_shape=(
                 jax.ShapeDtypeStruct((n_batch, tok, width), bf16),
                 jax.ShapeDtypeStruct((n_batch, seq + 1, heads, HEAD_DIM), bf16),
                 jax.ShapeDtypeStruct((n_batch, seq + 1, heads, HEAD_DIM), bf16),
+                jax.ShapeDtypeStruct((n_batch, width), bf16),
             ),
             in_specs=[
                 pl.BlockSpec((1, group_n, tok, cols), lambda b: (jnp.maximum(b, late), 0, 0, 0)),
@@ -580,11 +610,12 @@
                 pl.BlockSpec((1, 1, seq, cols), lambda b: (2, b, 0, 0)),
                 row((1, cols), (0, 0)),
                 row((1, cols), (0, 0)),
+                whole,
             ],
-            out_specs=(row((tok, width), (0, 0)), row((seq + 1, heads, HEAD_DIM), (0, 0, 0)), row((seq + 1, heads, HEAD_DIM), (0, 0, 0))),
+            out_specs=(row((tok, width), (0, 0)), cache, cache, whole),
             scratch_shapes=[pltpu.VMEM((width, width), bf16), pltpu.VMEM((tok, width), f32), dma],
             compiler_params=pltpu.CompilerParams(vmem_limit_bytes=VMEM_BYTES),
-        )(o_all, prompt_blk, w_o, post, out_early, qkv, qkv, k_new, v_new)
+        )(o_all, prompt_blk, w_o, post, out_early, qkv, qkv, k_new, v_new, out_d)
         return out_p, k_cache, v_cache, out_d
 
     replicated = P()

time: 383 us -> 377 us (0.984)
  Pallas kernels: 380 us -> 374 us
    pallas_call x1, Pallas kernels: 355 us -> 350 us  [device_step(): pl.pallas_call(functools.partial(exchange_kernel, group_n), out_shape=(ja...]
where the time goes in v6:
time: 377 us; the launch traced here: 376 us
  Pallas kernels  374 us (99%)
    pallas_call x1, Pallas kernels, device_step(): pl.pallas_call(functools.partial(exchange_kernel, group_n), out_shape=(ja...  350 us
    pallas_call x1, Pallas kernels, device_step(): pl.pallas_call(output_kernel, grid=(n_batch,), out_shape=(jax.ShapeDtypeS...  24.8 us

profile of v6, /device:TPU:81, one launch (start us, length us, event | category | flops | bytes accessed | tf_op | source)
XLA Modules:
  0.0 375.7 jit_solution(5620982276940115671)
XLA Ops:
  0.6 0.5 compare_select_fusion
  1.2 349.6 %shard_map.120 = (bf16[3,8,2048,256]{3,2,1,0:T(8,128)(2,1)}, bf16[8,8,256,256]{3,2,1,0:T(8,128)(2,1)}, bf16[8,2,2,2,256,256]{5,4,3,2,1,0:T(8,128)(2,1)}, bf16[8,...) custom-call(bf16[8,256,2048]{2,1,0:T(8,128)(2,1)} %x_ref.1, ...), custom_call_target="tpu_custom_call" | custom-call | tf_op jit(solution)/shard_map/pallas_call | solution.py:546
  350.8 24.8 %shard_map.121 = (bf16[8,256,2048]{2,1,0:T(8,128)(2,1)}, bf16[8,2049,2,128]{3,2,1,0:T(2,128)(2,1)}, bf16[8,2049,2,128]{3,2,1,0:T(2,128)(2,1)}, bf16[8,2048]{1,0:T(8,128)(2,1)}) custom-call(bf16[8,8,256,256]{3,2,1,0:T(8,128)(2,1)} %get-tuple-element.10.o_ref, bf16[8,256,2048]{2,1,0:T(8,128)(2,1)} %x_ref.1, bf16[2048,2048]{1,0:T(8,128)(2,1)} %wo_hbm.3, ...), custom_call_target="tpu_custom_call" | custom-call | tf_op jit(solution)/shard_map/pallas_call | solution.py:594

commit v7 on v6

--- a/solution.py
+++ b/solution.py
@@ -496,31 +496,35 @@
     width = group_n * cols
     heads = cols // HEAD_DIM
     b, n_batch = pl.program_id(0), pl.num_programs(0)
+    late = n_batch - LATE
+    first = late - LATE
     wo_copy = pltpu.make_async_copy(wo_hbm, wo_vm, wo_sem)
 
     @pl.when(b == 0)
     def _():
         wo_copy.start()
 
-    @pl.when(b < n_batch - LATE)
+    @pl.when(b < late)
     def _():
         out_ref[...] = outp_ref[...]
 
-    @pl.when(b == n_batch - LATE)
+    @pl.when(b == first)
     def _():
         wo_copy.wait()
 
-    @pl.when(b >= n_batch - LATE)
+    @pl.when(b >= first)
     def _():
+        which, half = (b - first) // 2, (b - first) % 2
         o_all = jnp.concatenate([o_ref[0, g] for g in range(group_n)], axis=1)
-        ssq = jnp.zeros((tok, 1), jnp.float32)
-        for n in range(width // COL_TILE):
-            at = slice(n * COL_TILE, (n + 1) * COL_TILE)
-            acc = jnp.dot(o_all, wo_vm[:, at], preferred_element_type=jnp.float32)
-            raw_vm[:, at] = acc
-            ssq = ssq + jnp.sum(acc * acc, axis=1, keepdims=True)
-        inv = lax.rsqrt(ssq / width + NORM_EPS)
-        out_ref[0] = (x_ref[0].astype(jnp.float32) + raw_vm[...] * inv * post_ref[...]).astype(jnp.bfloat16)
+        for n in range(width // 2 // COL_TILE):
+            at = pl.ds(pl.multiple_of(half * (width // 2) + n * COL_TILE, COL_TILE), COL_TILE)
+            raw_vm[which, :, at] = jnp.dot(o_all, wo_vm[:, at], preferred_element_type=jnp.float32)
+
+    @pl.when(b >= late)
+    def _():
+        rows = raw_vm[b - late]
+        inv = lax.rsqrt(jnp.sum(rows * rows, axis=1, keepdims=True) / width + NORM_EPS)
+        out_ref[0] = (x_ref[0].astype(jnp.float32) + rows * inv * post_ref[...]).astype(jnp.bfloat16)
 
     outd_ref[...] = outd_in_ref[...]
     seq = k_ref.shape[2]
@@ -601,7 +605,7 @@
                 jax.ShapeDtypeStruct((n_batch, width), bf16),
             ),
             in_specs=[
-                pl.BlockSpec((1, group_n, tok, cols), lambda b: (jnp.maximum(b, late), 0, 0, 0)),
+                pl.BlockSpec((1, group_n, tok, cols), lambda b: (late + b // late, 0, 0, 0)),
                 pl.BlockSpec((1, tok, width), lambda b: (jnp.maximum(b, late), 0, 0)),
                 any_spec,
                 vm_spec,
@@ -613,7 +617,7 @@
                 whole,
             ],
             out_specs=(row((tok, width), (0, 0)), cache, cache, whole),
-            scratch_shapes=[pltpu.VMEM((width, width), bf16), pltpu.VMEM((tok, width), f32), dma],
+            scratch_shapes=[pltpu.VMEM((width, width), bf16), pltpu.VMEM((LATE, tok, width), f32), dma],
             compiler_params=pltpu.CompilerParams(vmem_limit_bytes=VMEM_BYTES),
         )(o_all, prompt_blk, w_o, post, out_early, qkv, qkv, k_new, v_new, out_d)
         return out_p, k_cache, v_cache, out_d

time: 377 us -> 377 us (level)
  no operation moved by 1% of the time
where the time goes in v7:
time: 377 us; the launch traced here: 376 us
  Pallas kernels  375 us (99%)
    pallas_call x1, Pallas kernels, device_step(): pl.pallas_call(functools.partial(exchange_kernel, group_n), out_shape=(ja...  350 us
    pallas_call x1, Pallas kernels, device_step(): pl.pallas_call(output_kernel, grid=(n_batch,), out_shape=(jax.ShapeDtypeS...  25.4 us

profile of v7, /device:TPU:81, one launch (start us, length us, event | category | flops | bytes accessed | tf_op | source)
XLA Modules:
  0.0 376.4 jit_solution(11093581828103323251)
XLA Ops:
  0.6 0.5 compare_select_fusion
  1.2 349.6 %shard_map.120 = (bf16[3,8,2048,256]{3,2,1,0:T(8,128)(2,1)}, bf16[8,8,256,256]{3,2,1,0:T(8,128)(2,1)}, bf16[8,2,2,2,256,256]{5,4,3,2,1,0:T(8,128)(2,1)}, bf16[8,...) custom-call(bf16[8,256,2048]{2,1,0:T(8,128)(2,1)} %x_ref.1, ...), custom_call_target="tpu_custom_call" | custom-call | tf_op jit(solution)/shard_map/pallas_call | solution.py:550
  350.8 25.4 %shard_map.121 = (bf16[8,256,2048]{2,1,0:T(8,128)(2,1)}, bf16[8,2049,2,128]{3,2,1,0:T(2,128)(2,1)}, bf16[8,2049,2,128]{3,2,1,0:T(2,128)(2,1)}, bf16[8,2048]{1,0:T(8,128)(2,1)}) custom-call(bf16[8,8,256,256]{3,2,1,0:T(8,128)(2,1)} %get-tuple-element.10.o_ref, bf16[8,256,2048]{2,1,0:T(8,128)(2,1)} %x_ref.1, bf16[2048,2048]{1,0:T(8,128)(2,1)} %wo_hbm.3, ...), custom_call_target="tpu_custom_call" | custom-call | tf_op jit(solution)/shard_map/pallas_call | solution.py:598
